TPU v7x, 32 devices: a whole 2x2x4 slice. The times are simulated.
32 devices in a mesh: cube: 2 (over y), gz: 8 (over z, x), gy: 2 (over core).
Axes of the slice: x: 2, y: 2, z: 4, core: 2. Of those that a mesh axis runs over, the one named last changes fastest.
Arguments:
- noisy_cube: float32 [64, 64, 256], P(('cube', 'gz'), 'gy'), parts along dimension 0, may hold values from -40 to 40
- thresholds: float32 [4], replicated, may hold values from 0.5 to 4
Outputs:
- denoised: float32 [64, 4, 64, 256], P(('cube', 'gz'), None, 'gy'), parts along dimension 0
- gcv_score: float32 [8], P('cube'), parts along dimension 0
There are 2 independent parts, one for each index of `cube`. A program takes and returns all parts, laid end to end along the dimension named above; an argument that names none is the same for every part. Nothing has to cross between parts.
All inputs are finite; a program needn't handle non-finite values.
Results may differ from a plain program's by a relative error of at most 0.0003.
Values sent between devices are 32-bit elements; how exact they have to be, the bound alone decides.
No kernel may reach another device: no remote copies, remote signals or barrier semaphores. Data moves between devices by JAX's collectives and lax.ppermute only.
A program may use at most 64 MiB of HBM per device.

v0:
```python
import functools
import numpy as np
import jax
import jax.numpy as jnp
from jax import lax
from jax.experimental import pallas as pl
from jax.experimental.pallas import tpu as pltpu
from jax.sharding import PartitionSpec as P


LOWPASS = (
    0.2303778133088964,
    0.7148465705529155,
    0.6308807679298587,
    -0.0279837694168599,
    -0.1870348117190931,
    0.0308413818355607,
    0.0328830116668852,
    -0.010597401785069,
)
HIGHPASS = tuple((-1) ** tap * LOWPASS[7 - tap] for tap in range(8))
FILTERS = (LOWPASS, HIGHPASS)


def analysis_matrix(length):
    half = length // 2
    matrix = np.zeros((length, length))
    for band in range(2):
        for k in range(half):
            for tap in range(8):
                matrix[band * half + k, (2 * k + tap) % length] += FILTERS[band][tap]
    return matrix


def dot(a, b):
    return lax.dot_general(
        a, b, (((1,), (0,)), ((), ())),
        precision=lax.Precision.HIGHEST, preferred_element_type=jnp.float32,
    )


def weighted(terms):
    total = None
    for weight, value in terms:
        part = value * weight
        total = part if total is None else total + part
    return total


def depth_kernel(own_ref, before_ref, after_ref, out_ref):
    planes, rows, cols = own_ref.shape
    half_cols = cols // 2
    for r in range(0, rows, 8):
        for c in range(0, cols, half_cols):
            at = (pl.ds(r, 8), pl.ds(c, half_cols))
            tile = [before_ref[(i,) + at] for i in range(planes)]
            tile += [own_ref[(i,) + at] for i in range(planes)]
            tile += [after_ref[(i,) + at] for i in range(2)]
            for k in range(planes // 2):
                for band in range(2):
                    out_ref[(2 * k + band,) + at] = weighted(
                        (FILTERS[band][tap], tile[2 * k + tap]) for tap in range(8)
                    )


def tally(value, limit_squares, sums, keep=None):
    square = value * value
    for t, limit in enumerate(limit_squares):
        weight = 1.0 / (square + limit)
        cut = jnp.minimum(square, limit)
        if keep is not None:
            weight = jnp.where(keep, weight, 0.0)
            cut = jnp.where(keep, cut, 0.0)
        sums[0][t] = weight if sums[0][t] is None else sums[0][t] + weight
        sums[1][t] = cut if sums[1][t] is None else sums[1][t] + cut


def fold(sums):
    rows = [jnp.sum(a, axis=0, keepdims=True) for group in sums for a in group]
    return jnp.concatenate(rows, 0)


def plane_kernel(limits_ref, own_ref, other_ref, y_ref, x_ref, out_ref, tail_ref, parcel_ref, mid):
    planes, rows, cols = own_ref.shape
    out_rows = out_ref.shape[1]
    count = limits_ref.shape[0]
    squares = [limits_ref[t] * limits_ref[t] for t in range(count)]
    half_cols = cols // 2
    lo_rows = rows // 2
    for z in range(planes):
        plane = jnp.concatenate([own_ref[z], other_ref[z]], 0)
        mid[pl.ds(z * out_rows, out_rows), :] = dot(y_ref[...], plane)
    result = dot(mid[...], x_ref[...])
    for z in range(planes):
        out_ref[z] = result[z * out_rows : (z + 1) * out_rows]
    for z in range(2):
        tail_ref[z] = result[(planes - 2 + z) * out_rows : (planes - 1 + z) * out_rows]
    sums = [[None] * count, [None] * count]
    for z in range(planes):
        for r in range(0, 2 * lo_rows, 8):
            for c in range(0, cols, half_cols):
                value = result[z * out_rows + r : z * out_rows + r + 8, c : c + half_cols]
                if z % 2 == 0 and c == 0 and r < lo_rows:
                    parcel_ref[pl.ds(z // 2 * lo_rows + r, 8), :] = value
                else:
                    tally(value, squares, sums)
    parcel_ref[pl.ds(planes // 2 * lo_rows, 2 * count), :] = fold(sums)


def final_kernel(
    full, cells, index_ref, limits_ref, parcels_ref, own_ref, after_ref, tail_ref,
    ya_ref, xa_ref, ysa_ref, xsa_ref, ys_ref, xs_ref,
    out_ref, score_ref, zed, mix, coarse_in, coarse_mid, coarse, wide, wide_y,
):
    planes, rows, cols = own_ref.shape
    count = limits_ref.shape[0]
    half_cols = cols // 2
    limits = [limits_ref[t] for t in range(count)]
    squares = [t * t for t in limits]
    lo_rows = (parcels_ref.shape[2] - 2 * count) // (planes // 2)
    deep_rows = 2 * lo_rows
    pieces = parcels_ref.shape[1]
    depth = planes // 2
    kappas = list(range(-5, -5 + pieces)) if full else list(range(-5, 1))

    def coarse_plane(r, side, i):
        if full:
            r = r % (depth * pieces)
        at = index_ref[r // depth]
        return parcels_ref[side, at, pl.ds((r % depth) * lo_rows + i, 8), :]

    for side in range(2):
        for i in range(0, lo_rows, 8):
            needed = sorted({(2 * kap + 10 + tap) % (depth * pieces) if full else 2 * kap + 10 + tap
                             for kap in kappas for tap in range(8)})
            tile = {r: coarse_plane(r, side, i) for r in needed}
            for a, kap in enumerate(kappas):
                for band in range(2):
                    terms = []
                    for tap in range(8):
                        r = 2 * kap + 10 + tap
                        terms.append((FILTERS[band][tap], tile[r % (depth * pieces) if full else r]))
                    zed[2 * a + band, pl.ds(side * lo_rows + i, 8), :] = weighted(terms)
    for a in range(2 * len(kappas)):
        mix[pl.ds(a * deep_rows, deep_rows), :] = dot(ya_ref[...], zed[a])
    mix[...] = dot(mix[...], xa_ref[...])

    low_lanes = lax.broadcasted_iota(jnp.int32, (8, half_cols), 1) < half_cols // 2
    sums = [[None] * count, [None] * count]
    for a, kap in enumerate(kappas):
        if not full and kap != 0:
            continue
        for band in range(2):
            for i in range(0, deep_rows, 8):
                if not full and i % lo_rows >= lo_rows // 2:
                    continue
                kept = band == 0 and i < lo_rows
                value = mix[pl.ds((2 * a + band) * deep_rows + i, 8), :]
                tally(value, squares, sums, ~low_lanes if kept else None)
    total = fold(sums)
    if full:
        for side in range(2):
            for piece in range(pieces):
                total = total + parcels_ref[side, piece, pl.ds(depth * lo_rows, 2 * count), :]
    else:
        total = total + parcels_ref[0, index_ref[4], pl.ds(depth * lo_rows, 2 * count), :]
    for t in range(count):
        weight = jnp.sum(total[t : t + 1]) * squares[t]
        residual = jnp.sum(total[count + t : count + t + 1])
        if full:
            score_ref[t] = cells * residual / (weight * weight)
        else:
            score_ref[t] = weight
            score_ref[count + t] = residual

    back = [(-2, 1), (-1, 0), (-1, 1), (0, 0), (0, 1)]
    for t in range(count):
        for i in range(0, deep_rows, 8):
            shrunk = {}
            for a, kap in enumerate(kappas):
                if kap > 0:
                    continue
                for band in range(2):
                    value = mix[pl.ds((2 * a + band) * deep_rows + i, 8), :]
                    cut = value - jnp.clip(value, -limits[t], limits[t])
                    if band == 0 and i < lo_rows:
                        cut = jnp.where(low_lanes, value, cut)
                    shrunk[kap, band] = cut
            for b, (p, odd) in enumerate(back):
                coarse_in[t * 5 + b, pl.ds(i, 8), :] = weighted(
                    (FILTERS[band][2 * j + odd], shrunk[p - j, band])
                    for j in range(4) for band in range(2)
                )
    halo_rows = coarse.shape[1]
    for s in range(5 * count):
        coarse_mid[pl.ds(s * halo_rows, halo_rows), :] = dot(ysa_ref[...], coarse_in[s])
    spread = dot(coarse_mid[...], xsa_ref[...])
    for s in range(5 * count):
        coarse[s] = spread[s * halo_rows : (s + 1) * halo_rows]

    def source(kap, band, r, c):
        at = (pl.ds(r, 8), pl.ds(c, half_cols))
        if kap == -3:
            return tail_ref[(band,) + at]
        if kap < 0:
            return own_ref[(2 * (kap + 2) + band,) + at]
        return after_ref[(2 * kap + band,) + at]

    first = lax.broadcasted_iota(jnp.int32, (8, half_cols), 0) < 4
    for r in range(0, rows, 8):
        for c in range(0, cols, half_cols):
            for t in range(count):
                shrunk = {}
                for kap in range(-3, 2):
                    for band in range(2):
                        value = source(kap, band, r, c)
                        cut = value - jnp.clip(value, -limits[t], limits[t])
                        if band == 0 and c == 0:
                            if r < lo_rows:
                                cut = coarse[t * 5 + kap + 3, pl.ds(r, 8), :]
                            elif r >= 2 * lo_rows:
                                low = coarse[t * 5 + kap + 3, pl.ds(lo_rows, 8), :]
                                cut = jnp.where(first, low, cut)
                        shrunk[kap, band] = cut
                for z in range(planes):
                    wide[t * planes + z, pl.ds(r, 8), pl.ds(c, half_cols)] = weighted(
                        (FILTERS[band][2 * j + z % 2], shrunk[z // 2 - j, band])
                        for j in range(4) for band in range(2)
                    )
    y_rows = ys_ref.shape[0]
    for s in range(count * planes):
        wide_y[pl.ds(s * y_rows, y_rows), :] = dot(ys_ref[...], wide[s])
    result = dot(wide_y[...], xs_ref[...])
    for t in range(count):
        for z in range(planes):
            s = t * planes + z
            out_ref[z, t] = result[s * y_rows : (s + 1) * y_rows]


def shifted(array, axis, by):
    devices = lax.axis_size(axis)
    return lax.ppermute(array, axis, [(i, (i + by) % devices) for i in range(devices)])


VMEM = pl.BlockSpec(memory_space=pltpu.VMEM)
SMEM = pl.BlockSpec(memory_space=pltpu.SMEM)
PARAMS = pltpu.CompilerParams(vmem_limit_bytes=24 * 1024 * 1024)


def struct(*shape):
    return jax.ShapeDtypeStruct(shape, jnp.float32)


def constant(matrix):
    return jnp.asarray(np.ascontiguousarray(matrix), jnp.float32)


def body(noisy_cube, thresholds):
    planes, rows, cols = noisy_cube.shape
    count = thresholds.shape[0]
    n = lax.axis_size("gz")
    if lax.axis_size("gy") != 2 or planes != 4:
        raise ValueError("unsupported split")
    lo_rows = rows // 2
    pad = 4
    all_rows = 2 * lo_rows + 2 * pad
    full = n <= 8

    y_all = analysis_matrix(2 * rows)
    y_matrix = np.zeros((all_rows, 2 * rows))
    y_matrix[:lo_rows] = y_all[:lo_rows]
    y_matrix[lo_rows : 2 * lo_rows] = y_all[rows : rows + lo_rows]
    for band in range(2):
        start = 2 * lo_rows + band * pad
        stop = (band + 1) * rows
        y_matrix[start : start + 3] = y_all[stop - 3 : stop]
    x_matrix = analysis_matrix(cols)
    deep = analysis_matrix(rows)
    deep_x = analysis_matrix(cols // 2)
    picked = np.zeros((lo_rows + 8, rows))
    picked[:lo_rows] = deep[:, :lo_rows].T
    picked[lo_rows : lo_rows + 3] = deep[:, rows - 3 :].T

    ahead = shifted(noisy_cube, "gz", 1)
    behind = shifted(noisy_cube[:2], "gz", -1)
    layers = pl.pallas_call(
        depth_kernel,
        out_shape=struct(planes, rows, cols),
        in_specs=[VMEM] * 3,
        out_specs=VMEM,
        compiler_params=PARAMS,
        name="depth",
    )(noisy_cube, ahead, behind)
    other = shifted(layers, "gy", 1)
    own, tail, parcel = pl.pallas_call(
        plane_kernel,
        out_shape=(
            struct(planes, all_rows, cols),
            struct(2, all_rows, cols),
            struct(planes // 2 * lo_rows + 2 * count, cols // 2),
        ),
        in_specs=[SMEM] + [VMEM] * 4,
        out_specs=(VMEM,) * 3,
        scratch_shapes=[pltpu.VMEM((planes * all_rows, cols), jnp.float32)],
        compiler_params=PARAMS,
        name="plane",
    )(thresholds, layers, other, constant(y_matrix), constant(x_matrix.T))

    place = lax.axis_index("gz")
    offsets = jnp.arange(-4, 5)
    if full:
        pairs = n // 2
        column = [parcel]
        for q in range(1, pairs):
            column.append(shifted(parcel, "gz", -2 * q))
        column = jnp.stack(column)
        swapped = lax.ppermute(column, "gz", [(i, i ^ 1) for i in range(n)])
        side = jnp.concatenate([column, swapped])
        inside = place % 2
        spot = (inside + offsets) % n
        index = ((spot % 2) ^ inside) * pairs + spot // 2
    else:
        side = jnp.stack([parcel if o == 0 else shifted(parcel, "gz", -o) for o in range(-4, 5)])
        index = offsets + 4
    parcels = jnp.stack([side, shifted(side, "gy", 1)])
    before = shifted(tail, "gz", 1)
    after = shifted(own, "gz", -1)

    kappas = n if full else 6
    cells = float(planes * rows * cols * n * 2)
    denoised, score = pl.pallas_call(
        functools.partial(final_kernel, full, cells),
        out_shape=(
            struct(planes, count, rows, cols),
            struct(count if full else 2 * count),
        ),
        in_specs=[SMEM] * 2 + [VMEM] * 10,
        out_specs=(VMEM, SMEM),
        scratch_shapes=[
            pltpu.VMEM((2 * kappas, rows, cols // 2), jnp.float32),
            pltpu.VMEM((2 * kappas * rows, cols // 2), jnp.float32),
            pltpu.VMEM((5 * count, rows, cols // 2), jnp.float32),
            pltpu.VMEM((5 * count * (lo_rows + 8), cols // 2), jnp.float32),
            pltpu.VMEM((5 * count, lo_rows + 8, cols // 2), jnp.float32),
            pltpu.VMEM((count * planes, all_rows, cols), jnp.float32),
            pltpu.VMEM((count * planes * rows, cols), jnp.float32),
        ],
        compiler_params=PARAMS,
        name="final",
    )(
        index.astype(jnp.int32), thresholds, parcels, own, after, before,
        constant(deep), constant(deep_x.T), constant(picked), constant(deep_x),
        constant(y_matrix[:, :rows].T), constant(x_matrix),
    )
    if not full:
        total = lax.psum(score, ("gz", "gy"))
        score = cells * total[count:] / (total[:count] * total[:count])
    return denoised, score


def solution(mesh):
    in_specs = (P(("cube", "gz"), "gy", None), P())
    out_specs = (P(("cube", "gz"), None, "gy", None), P("cube"))
    return jax.shard_map(body, mesh=mesh, in_specs=in_specs, out_specs=out_specs, check_vma=False)
```

profile of v0, /device:TPU:0, one launch (start us, length us, event | category | flops | bytes accessed | tf_op | source)
XLA Modules:
  0.0 41.7 jit_solution(9875597502089651630)
XLA Ops:
  0.6 0.0 copy-start
  0.6 3.0 %collective-permute-start = (f32[4,32,256]{2,1,0:T(8,128)}, f32[4,32,256]{2,1,0:T(8,128)S(1)}, u32[]{:S(2)}, u32[]{:S(2)}) collective-permute-start(f32[4,32,256]{2,1,0:T(8,128)} %own_ref.1), channel_id=1, source_target_pairs={{0,2},{2,4},{4,6},{6,8},{8,10},{10,12},{12,14},{14,0},{1,3},{3,5},... | collective-permute-start | bytes 393224 | tf_op jit(solution)/shard_map/ppermute | solution.py:242
  3.7 0.9 %slice.3 = f32[2,32,256]{2,1,0:T(8,128)S(1)} slice(f32[4,32,256]{2,1,0:T(8,128)} %own_ref.1), slice={[0:2], [0:32], [0:256]} | slice | bytes 131072 | tf_op jit(solution)/shard_map/slice | solution.py:285
  4.5 0.0 copy-start.1
  4.5 0.0 copy-start.5
  4.5 0.0 copy-start.9
  4.6 3.1 %collective-permute-start.1 = (f32[2,32,256]{2,1,0:T(8,128)S(1)}, f32[2,32,256]{2,1,0:T(8,128)S(1)}, u32[]{:S(2)}, u32[]{:S(2)}) collective-permute-start(f32[2,32,256]{2,1,0:T(8,128)S(1)} %slice.3), channel_id=1, source_target_pairs={{0,14},{2,0},{4,2},{6,4},{8,6},{10,8},{12,10},{14,12},{1,15},{3,1}... | collective-permute-start | bytes 196616 | tf_op jit(solution)/shard_map/ppermute | solution.py:242
  7.7 3.5 %collective-permute-done.1.after_ref = f32[2,32,256]{2,1,0:T(8,128)S(1)} collective-permute-done((f32[2,32,256]{2,1,0:T(8,128)S(1)}, f32[2,32,256]{2,1,0:T(8,128)S(1)}, u32[]{:S(2)}, u32[]{:S(2)}) %collective-permute-start.1) | collective-permute-done | bytes 65568 | tf_op jit(solution)/shard_map/ppermute | solution.py:242
  11.1 0.0 collective-permute-done.before_ref
  11.1 0.0 copy-done
  11.1 0.1 depth.1.own_ref
  11.2 0.1 collective-permute-start.2
  11.3 1.3 %collective-permute-done.2.other_ref = f32[4,32,256]{2,1,0:T(8,128)S(1)} collective-permute-done((f32[4,32,256]{2,1,0:T(8,128)S(1)}, f32[4,32,256]{2,1,0:T(8,128)S(1)}, u32[]{:S(2)}, u32[]{:S(2)}) %collective-permute-start.2) | collective-permute-done | bytes 131104 | tf_op jit(solution)/shard_map/ppermute | solution.py:242
  12.6 0.0 copy-done.1
  12.6 0.0 copy-done.5
  12.6 0.0 copy-done.9
  12.6 1.1 %plane.1 = (f32[4,40,256]{2,1,0:T(8,128)S(1)}, f32[2,40,256]{2,1,0:T(8,128)S(1)}, f32[40,128]{1,0:T(8,128)S(1)}) custom-call(f32[4]{0:T(128)S(1)} %copy-done.9, f32[4,32,256]{2,1,0:T(8,128)S(1)} %depth.1.own_ref, f32[4,32,256]{2,1,0:T(8,128)S(1)} %collective-permute-done.2.other_ref, f32[40,64]{1,0:T(8,128)S(1)} %copy-done.5, f32[256,256]{1,0:T(8,128)S(1)} %copy-done.1), custom_call_target="tpu_custom_call" | custom-call | tf_op jit(solution)/shard_map/plane/pallas_call | solution.py:295
  13.8 0.4 %collective-permute-start.5 = (f32[40,128]{1,0:T(8,128)S(1)}, f32[40,128]{1,0:T(8,128)S(1)}, u32[]{:S(2)}, u32[]{:S(2)}) collective-permute-start(f32[40,128]{1,0:T(8,128)S(1)} %get-tuple-element.5), channel_id=1, source_target_pairs={{0,4},{2,6},{4,8},{6,10},{8,12},{10,14},{12,0},{14,2},{1,5},{3,7},... | collective-permute-start | bytes 61448 | tf_op jit(solution)/shard_map/ppermute | solution.py:242
  14.2 2.6 %collective-permute-start.4 = (f32[40,128]{1,0:T(8,128)S(1)}, f32[40,128]{1,0:T(8,128)S(1)}, u32[]{:S(2)}, u32[]{:S(2)}) collective-permute-start(f32[40,128]{1,0:T(8,128)S(1)} %get-tuple-element.5), channel_id=1, source_target_pairs={{0,8},{2,10},{4,12},{6,14},{8,0},{10,2},{12,4},{14,6},{1,9},{3,11}... | collective-permute-start | bytes 61448 | tf_op jit(solution)/shard_map/ppermute | solution.py:242
  16.8 1.3 %collective-permute-start.3 = (f32[40,128]{1,0:T(8,128)S(1)}, f32[40,128]{1,0:T(8,128)S(1)}, u32[]{:S(2)}, u32[]{:S(2)}) collective-permute-start(f32[40,128]{1,0:T(8,128)S(1)} %get-tuple-element.5), channel_id=1, source_target_pairs={{0,12},{2,14},{4,0},{6,2},{8,4},{10,6},{12,8},{14,10},{1,13},{3,15... | collective-permute-start | bytes 61448 | tf_op jit(solution)/shard_map/ppermute | solution.py:242
  18.1 1.3 %collective-permute-done.5 = f32[40,128]{1,0:T(8,128)S(1)} collective-permute-done((f32[40,128]{1,0:T(8,128)S(1)}, f32[40,128]{1,0:T(8,128)S(1)}, u32[]{:S(2)}, u32[]{:S(2)}) %collective-permute-start.5) | collective-permute-done | bytes 20512 | tf_op jit(solution)/shard_map/ppermute | solution.py:242
  19.4 0.0 collective-permute-done.4
  19.4 1.2 %collective-permute-done.3 = f32[40,128]{1,0:T(8,128)S(1)} collective-permute-done((f32[40,128]{1,0:T(8,128)S(1)}, f32[40,128]{1,0:T(8,128)S(1)}, u32[]{:S(2)}, u32[]{:S(2)}) %collective-permute-start.3) | collective-permute-done | bytes 20512 | tf_op jit(solution)/shard_map/ppermute | solution.py:242
  20.6 1.7 %collective-permute-start.6 = (f32[4,40,128]{2,1,0:T(8,128)S(1)}, f32[4,40,128]{2,1,0:T(8,128)S(1)}, u32[]{:S(2)}, u32[]{:S(2)}) collective-permute-start(f32[4,40,128]{2,1,0:T(8,128)S(1)} %pad_maximum_fusion.1), channel_id=1, source_target_pairs={{0,2},{2,0},{4,6},{6,4},{8,10},{10,8},{12,14},{14,12},{1,3},{3,1},... | collective-permute-start | bytes 245768 | tf_op jit(solution)/shard_map/ppermute | solution.py:317
  22.3 2.8 %collective-permute-done.6 = f32[4,40,128]{2,1,0:T(8,128)S(1)} collective-permute-done((f32[4,40,128]{2,1,0:T(8,128)S(1)}, f32[4,40,128]{2,1,0:T(8,128)S(1)}, u32[]{:S(2)}, u32[]{:S(2)}) %collective-permute-start.6) | collective-permute-done | bytes 81952 | tf_op jit(solution)/shard_map/ppermute | solution.py:317
  25.1 0.1 collective-permute-start.7
  25.2 4.0 %collective-permute-start.8 = (f32[4,40,256]{2,1,0:T(8,128)S(1)}, f32[4,40,256]{2,1,0:T(8,128)S(1)}, u32[]{:S(2)}, u32[]{:S(2)}) collective-permute-start(f32[4,40,256]{2,1,0:T(8,128)S(1)} %get-tuple-element.6.own_ref), channel_id=1, source_target_pairs={{0,14},{2,0},{4,2},{6,4},{8,6},{10,8},{12,10},{14,12},{1,15},{3,1}... | collective-permute-start | bytes 491528 | tf_op jit(solution)/shard_map/ppermute | solution.py:242
  29.2 0.1 collective-permute-start.9
  29.3 0.0 collective-permute-done.7
  29.3 0.0 copy-start.2
  29.3 0.0 copy-start.3
  29.3 0.0 copy-start.4
  29.4 0.0 copy-start.6
  29.4 0.0 copy-start.7
  29.4 0.0 copy-start.8
  29.4 7.1 %collective-permute-done.9.tail_ref = f32[2,40,256]{2,1,0:T(8,128)S(1)} collective-permute-done((f32[2,40,256]{2,1,0:T(8,128)S(1)}, f32[2,40,256]{2,1,0:T(8,128)S(1)}, u32[]{:S(2)}, u32[]{:S(2)}) %collective-permute-start.9) | collective-permute-done | bytes 81952 | tf_op jit(solution)/shard_map/ppermute | solution.py:242
  36.5 0.0 collective-permute-done.8.after_ref
  36.5 0.0 copy-done.2
  36.5 0.0 copy-done.3
  36.5 0.0 copy-done.4
  36.5 0.0 copy-done.6
  36.5 0.0 copy-done.7
  36.5 0.0 copy-done.8
  36.5 5.1 %final.1 = (f32[4,4,32,256]{3,2,1,0:T(8,128)}, f32[4]{0:T(128)}) custom-call(s32[9]{0:T(128)S(1)} %fusion.2.index_ref, f32[4]{0:T(128)S(1)} %copy-done.9, f32[2,8,40,128]{3,2,1,0:T(8,128)S(1)} %pad_maximum_fusion.parcels_ref, f32[4,40,256]{2,1,0:T(8,128)S(1)} %get-tuple-element.6.own_ref, f32[4,40,256]{2,1,0:T(8,128)S(1)} %collective-permute-done.8.after_ref, ...), custom_call_target="tpu_custom_call" | custom-call | tf_op jit(solution)/shard_map/final/pallas_call | solution.py:331
  (8 shorter events, 0.1 us)
Async XLA Ops:
  0.6 10.5 %copy-start = (f32[4,32,256]{2,1,0:T(8,128)S(1)}, f32[4,32,256]{2,1,0:T(8,128)}, u32[]{:S(2)}) copy-start(f32[4,32,256]{2,1,0:T(8,128)} %own_ref.1) | copy-start | bytes 393220
  0.6 10.5 %collective-permute-start = (f32[4,32,256]{2,1,0:T(8,128)}, f32[4,32,256]{2,1,0:T(8,128)S(1)}, u32[]{:S(2)}, u32[]{:S(2)}) collective-permute-start(f32[4,32,256]{2,1,0:T(8,128)} %own_ref.1), channel_id=1, source_target_pairs={{0,2},{2,4},{4,6},{6,8},{8,10},{10,12},{12,14},{14,0},{1,3},{3,5},... | collective-permute-start | bytes 393224 | tf_op jit(solution)/shard_map/ppermute | solution.py:242
  4.5 8.1 %copy-start.1 = (f32[256,256]{1,0:T(8,128)S(1)}, f32[256,256]{1,0:T(8,128)}, u32[]{:S(2)}) copy-start(f32[256,256]{1,0:T(8,128)} %constant.70.clone.x_ref) | copy-start | bytes 786436
  4.5 8.1 %copy-start.5 = (f32[40,64]{1,0:T(8,128)S(1)}, f32[40,64]{1,0:T(8,128)}, u32[]{:S(2)}) copy-start(f32[40,64]{1,0:T(8,128)} %constant.69.clone.y_ref) | copy-start | bytes 30724
  4.5 8.1 %copy-start.9 = (f32[4]{0:T(128)S(1)}, f32[4]{0:T(128)}, u32[]{:S(2)}) copy-start(f32[4]{0:T(128)} %limits_ref.3) | copy-start | bytes 52
  4.6 6.6 %collective-permute-start.1 = (f32[2,32,256]{2,1,0:T(8,128)S(1)}, f32[2,32,256]{2,1,0:T(8,128)S(1)}, u32[]{:S(2)}, u32[]{:S(2)}) collective-permute-start(f32[2,32,256]{2,1,0:T(8,128)S(1)} %slice.3), channel_id=1, source_target_pairs={{0,14},{2,0},{4,2},{6,4},{8,6},{10,8},{12,10},{14,12},{1,15},{3,1}... | collective-permute-start | bytes 196616 | tf_op jit(solution)/shard_map/ppermute | solution.py:242
  11.2 1.4 %collective-permute-start.2 = (f32[4,32,256]{2,1,0:T(8,128)S(1)}, f32[4,32,256]{2,1,0:T(8,128)S(1)}, u32[]{:S(2)}, u32[]{:S(2)}) collective-permute-start(f32[4,32,256]{2,1,0:T(8,128)S(1)} %depth.1.own_ref), channel_id=1, source_target_pairs={{0,1},{1,0},{2,3},{3,2},{4,5},{5,4},{6,7},{7,6},{8,9},{9,8},{10,11... | collective-permute-start | bytes 393224 | tf_op jit(solution)/shard_map/ppermute | solution.py:242
  13.8 5.6 %collective-permute-start.5 = (f32[40,128]{1,0:T(8,128)S(1)}, f32[40,128]{1,0:T(8,128)S(1)}, u32[]{:S(2)}, u32[]{:S(2)}) collective-permute-start(f32[40,128]{1,0:T(8,128)S(1)} %get-tuple-element.5), channel_id=1, source_target_pairs={{0,4},{2,6},{4,8},{6,10},{8,12},{10,14},{12,0},{14,2},{1,5},{3,7},... | collective-permute-start | bytes 61448 | tf_op jit(solution)/shard_map/ppermute | solution.py:242
  14.2 5.2 %collective-permute-start.4 = (f32[40,128]{1,0:T(8,128)S(1)}, f32[40,128]{1,0:T(8,128)S(1)}, u32[]{:S(2)}, u32[]{:S(2)}) collective-permute-start(f32[40,128]{1,0:T(8,128)S(1)} %get-tuple-element.5), channel_id=1, source_target_pairs={{0,8},{2,10},{4,12},{6,14},{8,0},{10,2},{12,4},{14,6},{1,9},{3,11}... | collective-permute-start | bytes 61448 | tf_op jit(solution)/shard_map/ppermute | solution.py:242
  16.8 3.8 %collective-permute-start.3 = (f32[40,128]{1,0:T(8,128)S(1)}, f32[40,128]{1,0:T(8,128)S(1)}, u32[]{:S(2)}, u32[]{:S(2)}) collective-permute-start(f32[40,128]{1,0:T(8,128)S(1)} %get-tuple-element.5), channel_id=1, source_target_pairs={{0,12},{2,14},{4,0},{6,2},{8,4},{10,6},{12,8},{14,10},{1,13},{3,15... | collective-permute-start | bytes 61448 | tf_op jit(solution)/shard_map/ppermute | solution.py:242
  20.6 4.5 %collective-permute-start.6 = (f32[4,40,128]{2,1,0:T(8,128)S(1)}, f32[4,40,128]{2,1,0:T(8,128)S(1)}, u32[]{:S(2)}, u32[]{:S(2)}) collective-permute-start(f32[4,40,128]{2,1,0:T(8,128)S(1)} %pad_maximum_fusion.1), channel_id=1, source_target_pairs={{0,2},{2,0},{4,6},{6,4},{8,10},{10,8},{12,14},{14,12},{1,3},{3,1},... | collective-permute-start | bytes 245768 | tf_op jit(solution)/shard_map/ppermute | solution.py:317
  25.1 4.2 %collective-permute-start.7 = (f32[8,40,128]{2,1,0:T(8,128)S(1)}, f32[8,40,128]{2,1,0:T(8,128)S(1)}, u32[]{:S(2)}, u32[]{:S(2)}) collective-permute-start(f32[8,40,128]{2,1,0:T(8,128)S(1)} %constant_dynamic-update-slice_fusion), channel_id=1, source_target_pairs={{0,1},{1,0},{2,3},{3,2},{4,5},{5,4},{6,7},{7,6},{8,9},{9,8},{10,11... | collective-permute-start | bytes 491528 | tf_op jit(solution)/shard_map/ppermute | solution.py:242
  25.2 11.3 %collective-permute-start.8 = (f32[4,40,256]{2,1,0:T(8,128)S(1)}, f32[4,40,256]{2,1,0:T(8,128)S(1)}, u32[]{:S(2)}, u32[]{:S(2)}) collective-permute-start(f32[4,40,256]{2,1,0:T(8,128)S(1)} %get-tuple-element.6.own_ref), channel_id=1, source_target_pairs={{0,14},{2,0},{4,2},{6,4},{8,6},{10,8},{12,10},{14,12},{1,15},{3,1}... | collective-permute-start | bytes 491528 | tf_op jit(solution)/shard_map/ppermute | solution.py:242
  29.2 7.3 %collective-permute-start.9 = (f32[2,40,256]{2,1,0:T(8,128)S(1)}, f32[2,40,256]{2,1,0:T(8,128)S(1)}, u32[]{:S(2)}, u32[]{:S(2)}) collective-permute-start(f32[2,40,256]{2,1,0:T(8,128)S(1)} %get-tuple-element.7), channel_id=1, source_target_pairs={{0,2},{2,4},{4,6},{6,8},{8,10},{10,12},{12,14},{14,0},{1,3},{3,5},... | collective-permute-start | bytes 245768 | tf_op jit(solution)/shard_map/ppermute | solution.py:242
  29.3 7.2 %copy-start.2 = (f32[256,256]{1,0:T(8,128)S(1)}, f32[256,256]{1,0:T(8,128)}, u32[]{:S(2)}) copy-start(f32[256,256]{1,0:T(8,128)} %constant.76.clone.xs_ref) | copy-start | bytes 786436
  29.3 7.2 %copy-start.3 = (f32[128,128]{1,0:T(8,128)S(1)}, f32[128,128]{1,0:T(8,128)}, u32[]{:S(2)}) copy-start(f32[128,128]{1,0:T(8,128)} %constant.74.clone.xsa_ref) | copy-start | bytes 196612
  29.3 7.2 %copy-start.4 = (f32[128,128]{1,0:T(8,128)S(1)}, f32[128,128]{1,0:T(8,128)}, u32[]{:S(2)}) copy-start(f32[128,128]{1,0:T(8,128)} %constant.72.clone.xa_ref) | copy-start | bytes 196612
  29.4 7.2 %copy-start.6 = (f32[32,40]{1,0:T(8,128)S(1)}, f32[32,40]{1,0:T(8,128)}, u32[]{:S(2)}) copy-start(f32[32,40]{1,0:T(8,128)} %constant.75.clone.ys_ref) | copy-start | bytes 15364
  29.4 7.2 %copy-start.7 = (f32[32,32]{1,0:T(8,128)S(1)}, f32[32,32]{1,0:T(8,128)}, u32[]{:S(2)}) copy-start(f32[32,32]{1,0:T(8,128)} %constant.71.clone.ya_ref) | copy-start | bytes 12292
  29.4 7.2 %copy-start.8 = (f32[24,32]{1,0:T(8,128)S(1)}, f32[24,32]{1,0:T(8,128)}, u32[]{:S(2)}) copy-start(f32[24,32]{1,0:T(8,128)} %constant.73.clone.ysa_ref) | copy-start | bytes 9220
where the time goes:
time: 41.8 us; the launch traced here: 41.7 us
  waiting for transfers between devices  17.1 us (41%)
  starting transfers between devices  16.5 us (39%)
  Pallas kernels  6.32 us (15%)
  local copies, waits for them, and re-layouts  0.95 us (2%)
  between operations  0.81 us (2%)
    ppermute x9, starting transfers between devices, shifted(): lax.ppermute(array, axis, [(i, (i + by) % devices) for i in range(devices)])  14.7 us
    ppermute x9, waiting for transfers between devices, shifted(): lax.ppermute(array, axis, [(i, (i + by) % devices) for i in range(devices)])  14.3 us
    pallas_call x1, Pallas kernels, body(): pl.pallas_call(functools.partial(final_kernel, full, cells), out_shape=(s...  5.11 us
    ppermute x1, waiting for transfers between devices, body(): swapped = lax.ppermute(column, 'gz', [(i, i ^ 1) for i in range(n)])  2.77 us
    ppermute x1, starting transfers between devices, body(): swapped = lax.ppermute(column, 'gz', [(i, i ^ 1) for i in range(n)])  1.72 us
    pallas_call x1, Pallas kernels, body(): pl.pallas_call(plane_kernel, out_shape=(struct(planes, all_rows, cols), s...  1.14 us
    slice x1, local copies, waits for them, and re-layouts, body(): behind = shifted(noisy_cube[:2], 'gz', -1)  0.88 us
  transfers between devices with their start and end apart: 10, of which 6 were waited for; matrix products, arithmetic and copies ran while one was open for 2% of the time, Pallas kernels for 0%

commit v1 on v0

v1 whole, which is shorter than its diff:
```python
import functools
import jax
import jax.numpy as jnp
from jax import lax
from jax.experimental import pallas as pl
from jax.experimental.pallas import tpu as pltpu
from jax.sharding import PartitionSpec as P


LOWPASS = (
    0.2303778133088964,
    0.7148465705529155,
    0.6308807679298587,
    -0.0279837694168599,
    -0.1870348117190931,
    0.0308413818355607,
    0.0328830116668852,
    -0.010597401785069,
)
HIGHPASS = tuple((-1) ** tap * LOWPASS[7 - tap] for tap in range(8))
FILTERS = (LOWPASS, HIGHPASS)
EDGE = 8


def dot(a, b, contract=0):
    return lax.dot_general(
        a, b, (((1,), (contract,)), ((), ())),
        precision=lax.Precision.HIGHEST, preferred_element_type=jnp.float32,
    )


def weighted(terms):
    total = None
    for weight, value in terms:
        part = value * weight
        total = part if total is None else total + part
    return total


def filter_tile(first, position, length, band):
    gap = position - first
    gap = jnp.where(gap < 0, gap + length, gap)
    value = jnp.zeros(gap.shape, jnp.float32)
    for tap in range(8):
        value = jnp.where(gap == tap, FILTERS[band][tap], value)
    return value


def iota(shape, dimension):
    return lax.broadcasted_iota(jnp.int32, shape, dimension)


def edge_rows(row, last):
    return last - 2 + row % 4


def analysis_tiles(ref):
    length = ref.shape[0]
    half = length // 2
    for band in range(2):
        shape = (half, length)
        ref[pl.ds(band * half, half), :] = filter_tile(2 * iota(shape, 0), iota(shape, 1), length, band)


def blocks(shape, block):
    row, column = iota(shape, 0), iota(shape, 1)
    return row % block, column % block, row // block == column // block


def first_kernel(cube_ref, x_ref, y_ref, cube_out_ref, semaphore):
    copy = pltpu.make_async_copy(cube_ref, cube_out_ref, semaphore)
    copy.start()
    rows, length = y_ref.shape
    half = rows // 2
    for band in range(2):
        shape = (half, length)
        y_ref[pl.ds(band * half, half), :] = filter_tile(2 * iota(shape, 0), iota(shape, 1), length, band)
    analysis_tiles(x_ref)
    copy.wait()


def second_kernel(x_ref, deep_x_ref, both_x_ref, back_y_ref, deep_y_ref, both_y_ref):
    half_cols = deep_x_ref.shape[0]
    analysis_tiles(deep_x_ref)
    both_x_ref[...] = dot(deep_x_ref[...], x_ref[pl.ds(0, half_cols), :])
    shape = back_y_ref.shape
    rows = shape[0]
    half = rows // 2
    sample, column = iota(shape, 0), iota(shape, 1)
    total = jnp.zeros(shape, jnp.float32)
    for band in range(2):
        value = filter_tile(2 * (column - band * half), sample, 2 * rows, band)
        total = jnp.where((column >= band * half) & (column < (band + 1) * half), value, total)
        start = rows + band * 4
        value = filter_tile(2 * edge_rows(column - start, -1), sample, 2 * rows, band)
        total = jnp.where((column >= start) & (column < start + 3), value, total)
    back_y_ref[...] = total
    row, column, mask = blocks(deep_y_ref.shape, rows)
    first = 2 * jnp.where(row < half, row, row - half)
    lo = filter_tile(first, column, rows, 0)
    hi = filter_tile(first, column, rows, 1)
    deep_y_ref[...] = jnp.where(mask, jnp.where(row < half, lo, hi), 0.0)
    lows = jnp.where(mask, filter_tile(2 * column, row, 2 * rows, 0), 0.0)
    both_y_ref[...] = dot(lows, deep_y_ref[...], 1)


def plane_kernel(flags_ref, own_ref, other_ref, y_ref, x_ref, out_ref, far_ref, mid):
    planes, rows, _ = own_ref.shape
    for z in range(planes):
        plane = jnp.concatenate([own_ref[z], other_ref[z]], 0)
        mid[pl.ds(z * rows, rows), :] = dot(y_ref[...], plane)
    result = dot(mid[...], x_ref[...], 1)
    odd = flags_ref[0] == 1
    for z in range(planes):
        out_ref[z] = result[z * rows : (z + 1) * rows]
    for z in range(2):
        head = result[z * rows : (z + 1) * rows]
        tail = result[(planes - 2 + z) * rows : (planes - 1 + z) * rows]
        far_ref[z] = jnp.where(odd, head, tail)


def tally(value, limit_squares, sums, keep=None):
    square = value * value
    for t, limit in enumerate(limit_squares):
        weight = 1.0 / (square + limit)
        cut = jnp.minimum(square, limit)
        if keep is not None:
            weight = jnp.where(keep, weight, 0.0)
            cut = jnp.where(keep, cut, 0.0)
        sums[0][t] = weight if sums[0][t] is None else sums[0][t] + weight
        sums[1][t] = cut if sums[1][t] is None else sums[1][t] + cut


def fold(sums):
    rows = [jnp.sum(a, axis=0, keepdims=True) for group in sums for a in group]
    return jnp.concatenate(rows, 0)


def depth_kernel(flags_ref, limits_ref, own_ref, mate_ref, level_ref, deep_x_ref, parcel_ref, lows):
    planes, rows, cols = own_ref.shape
    count = limits_ref.shape[0]
    squares = [limits_ref[t] * limits_ref[t] for t in range(count)]
    half_cols = cols // 2
    lo_rows = rows // 2
    odd = flags_ref[0] == 1
    sums = [[None] * count, [None] * count]
    for r in range(0, rows, 8):
        for c in range(0, cols, half_cols):
            at = (pl.ds(r, 8), pl.ds(c, half_cols))
            own = [own_ref[(i,) + at] for i in range(planes)]
            level = [level_ref[(i,) + at] for i in range(planes)]
            tile = [jnp.where(odd, level[i], own[i]) for i in range(planes)]
            tile += [mate_ref[(i,) + at] for i in range(planes)]
            tile += [jnp.where(odd, own[i], level[i]) for i in range(2)]
            for k in range(planes // 2):
                for band in range(2):
                    value = weighted((FILTERS[band][tap], tile[2 * k + tap]) for tap in range(8))
                    if band == 0 and c == 0 and r < lo_rows:
                        lows[pl.ds(k * lo_rows + r, 8), :] = value
                    else:
                        tally(value, squares, sums)
    parcel_ref[pl.ds(0, planes // 2 * lo_rows), :] = dot(lows[...], deep_x_ref[...], 1)
    parcel_ref[pl.ds(planes // 2 * lo_rows, 2 * count), :] = fold(sums)


def stack_kernel(flags_ref, own_ref, mate_ref, level_ref, cross_ref, far_ref, out_ref, edge_ref):
    planes, rows, cols = own_ref.shape
    half_cols = cols // 2
    odd = flags_ref[0] == 1
    for r in range(0, rows, 8):
        for c in range(0, cols, half_cols):
            at = (pl.ds(r, 8), pl.ds(c, half_cols))
            mate = [mate_ref[(i,) + at] for i in range(planes)]
            cross = [cross_ref[(i,) + at] for i in range(planes)]
            level = [level_ref[(i,) + at] for i in range(planes)]
            far = [far_ref[(i,) + at] for i in range(2)]
            tile = [jnp.where(odd, level[planes - 2 + i], far[i]) for i in range(2)]
            tile += [jnp.where(odd, mate[i], cross[i]) for i in range(planes)]
            tile += [own_ref[(i,) + at] for i in range(planes)]
            tile += [jnp.where(odd, cross[i], mate[i]) for i in range(planes)]
            tile += [jnp.where(odd, far[i], level[i]) for i in range(2)]
            for k in range(5):
                for band in range(2):
                    value = weighted((FILTERS[band][tap], tile[2 * k + tap]) for tap in range(8))
                    out_ref[(2 * k + band,) + at] = value
    edge_ref[...] = jnp.zeros(edge_ref.shape, jnp.float32)
    for k in range(10):
        for band in range(2):
            stop = (band + 1) * rows // 2
            edge_ref[k, pl.ds(band * 4, 3), :] = out_ref[k, pl.ds(stop - 3, 3), :]


def detail_kernel(limits_ref, coefs_ref, edge_ref, back_y_ref, x_ref, out_ref, wide, wide_y):
    count, planes = out_ref.shape[0], out_ref.shape[1]
    _, rows, cols = coefs_ref.shape
    half_cols = cols // 2
    lo_rows = rows // 2
    limits = [limits_ref[t] for t in range(count)]
    low_edge = iota((8, half_cols), 0) < 4
    for r in range(0, rows + EDGE, 8):
        for c in range(0, cols, half_cols):
            if r < rows:
                tile = [coefs_ref[i, pl.ds(r, 8), pl.ds(c, half_cols)] for i in range(10)]
            else:
                tile = [edge_ref[i, :, pl.ds(c, half_cols)] for i in range(10)]
            for t in range(count):
                shrunk = {}
                for i, value in enumerate(tile):
                    kap, band = i // 2 - 3, i % 2
                    if band == 0 and c == 0 and r < lo_rows:
                        continue
                    cut = value - jnp.clip(value, -limits[t], limits[t])
                    if band == 0 and c == 0 and r >= rows:
                        cut = jnp.where(low_edge, 0.0, cut)
                    shrunk[kap, band] = cut
                for z in range(planes):
                    wide[t * planes + z, pl.ds(r, 8), pl.ds(c, half_cols)] = weighted(
                        (FILTERS[band][2 * j + z % 2], shrunk[z // 2 - j, band])
                        for j in range(4) for band in range(2) if (z // 2 - j, band) in shrunk
                    )
    for s in range(count * planes):
        wide_y[pl.ds(s * rows, rows), :] = dot(back_y_ref[...], wide[s])
    result = dot(wide_y[...], x_ref[...])
    for t in range(count):
        for z in range(planes):
            s = t * planes + z
            out_ref[t, z] = result[s * rows : (s + 1) * rows]


def way_back(z):
    weights = {}
    for i in range(4):
        plane = z // 2 - i
        for j in range(4):
            for band in range(2):
                at = (plane // 2 - j, band)
                weights[at] = weights.get(at, 0.0) + LOWPASS[2 * i + z % 2] * FILTERS[band][2 * j + plane % 2]
    return weights


def final_kernel(
    full, cells, index_ref, limits_ref, parcels_ref, detail_ref, deep_y_ref, both_y_ref, both_x_ref,
    out_ref, score_ref, zed, mix, coarse,
):
    count, planes, rows, cols = detail_ref.shape
    half_cols = cols // 2
    limits = [limits_ref[t] for t in range(count)]
    squares = [t * t for t in limits]
    depth = planes // 2
    lo_rows = (parcels_ref.shape[2] - 2 * count) // depth
    deep_rows = 2 * lo_rows
    pieces = parcels_ref.shape[1]
    kappas = list(range(-5, -5 + pieces)) if full else list(range(-5, 1))

    def place(kap, tap):
        r = 2 * kap + 10 + tap
        return r % (depth * pieces) if full else r

    for side in range(2):
        for i in range(0, lo_rows, 8):
            tile = {}
            for r in sorted({place(kap, tap) for kap in kappas for tap in range(8)}):
                tile[r] = parcels_ref[side, index_ref[r // depth], pl.ds((r % depth) * lo_rows + i, 8), :]
            for a, kap in enumerate(kappas):
                for band in range(2):
                    zed[pl.ds((2 * a + band) * deep_rows + side * lo_rows + i, 8), :] = weighted(
                        (FILTERS[band][tap], tile[place(kap, tap)]) for tap in range(8)
                    )
    block = deep_y_ref.shape[0]
    for a in range(0, zed.shape[0], block):
        mix[pl.ds(a, block), :] = dot(deep_y_ref[...], zed[pl.ds(a, block), :])

    low_lanes = iota((8, half_cols), 1) < half_cols // 2
    for t in range(count):
        for i in range(0, deep_rows, 8):
            shrunk = {}
            for a, kap in enumerate(kappas):
                if kap > 0:
                    continue
                for band in range(2):
                    value = mix[pl.ds((2 * a + band) * deep_rows + i, 8), :]
                    cut = value - jnp.clip(value, -limits[t], limits[t])
                    if band == 0 and i < lo_rows:
                        cut = jnp.where(low_lanes, value, cut)
                    shrunk[kap, band] = cut
            for z in range(planes):
                coarse[pl.ds((t * planes + z) * rows + i, 8), :] = weighted(
                    (weight, shrunk[at]) for at, weight in way_back(z).items()
                )
        result = dot(both_y_ref[...], coarse[pl.ds(t * block, block), :])
        result = dot(result, both_x_ref[...])
        for z in range(planes):
            out_ref[z, t] = detail_ref[t, z] + result[z * rows : (z + 1) * rows]

    sums = [[None] * count, [None] * count]
    for a, kap in enumerate(kappas):
        if not full and kap != 0:
            continue
        for band in range(2):
            for i in range(0, deep_rows, 8):
                if not full and i % lo_rows >= lo_rows // 2:
                    continue
                kept = band == 0 and i < lo_rows
                value = mix[pl.ds((2 * a + band) * deep_rows + i, 8), :]
                tally(value, squares, sums, ~low_lanes if kept else None)
    total = fold(sums)
    if full:
        for side in range(2):
            for piece in range(pieces):
                total = total + parcels_ref[side, piece, pl.ds(depth * lo_rows, 2 * count), :]
    else:
        total = total + parcels_ref[0, 5, pl.ds(depth * lo_rows, 2 * count), :]
    for t in range(count):
        weight = jnp.sum(total[t : t + 1]) * squares[t]
        residual = jnp.sum(total[count + t : count + t + 1])
        if full:
            score_ref[t] = cells * residual / (weight * weight)
        else:
            score_ref[t] = weight
            score_ref[count + t] = residual


def shifted(array, axis, by):
    devices = lax.axis_size(axis)
    return lax.ppermute(array, axis, [(i, (i + by) % devices) for i in range(devices)])


def exchanged(array, partner):
    devices = lax.axis_size("gz")
    return lax.ppermute(array, "gz", [(i, partner(i) % devices) for i in range(devices)])


VMEM = pl.BlockSpec(memory_space=pltpu.VMEM)
SMEM = pl.BlockSpec(memory_space=pltpu.SMEM)
PARAMS = pltpu.CompilerParams(vmem_limit_bytes=24 * 1024 * 1024)


def struct(*shape):
    return jax.ShapeDtypeStruct(shape, jnp.float32)


def scratch(*shape):
    return pltpu.VMEM(shape, jnp.float32)


def call(kernel, out_shape, smem, vmem, scratches=(), score=False, flops=100_000):
    out_specs = jax.tree.map(lambda _: VMEM, out_shape)
    if score:
        out_specs = (VMEM, SMEM)

    def run(*operands):
        return pl.pallas_call(
            kernel,
            out_shape=out_shape,
            in_specs=[SMEM] * smem + vmem,
            out_specs=out_specs,
            scratch_shapes=list(scratches),
            compiler_params=PARAMS,
            cost_estimate=pl.CostEstimate(flops=flops, bytes_accessed=0, transcendentals=0),
        )(*operands)

    return run


def body(noisy_cube, thresholds):
    planes, rows, cols = noisy_cube.shape
    count = thresholds.shape[0]
    n = lax.axis_size("gz")
    if lax.axis_size("gy") != 2 or planes != 4 or n % 4:
        raise ValueError("unsupported split")
    lo_rows = rows // 2
    half_cols = cols // 2
    full = n <= 8 and n & (n - 1) == 0

    place = lax.axis_index("gz")
    inside = place % 2
    flags = inside.astype(jnp.int32)[None]

    other = shifted(noisy_cube, "gy", 1)
    x_matrix, y_matrix, cube = call(
        first_kernel,
        (
            struct(cols, cols), struct(rows, 2 * rows), struct(planes, rows, cols),
        ), 0, [pl.BlockSpec(memory_space=pltpu.HBM)], [pltpu.SemaphoreType.DMA],
    )(noisy_cube)
    flat, far = call(
        plane_kernel, (struct(planes, rows, cols), struct(2, rows, cols)), 1, [VMEM] * 4,
        [scratch(planes * rows, cols)],
    )(flags, cube, other, y_matrix, x_matrix)

    level = exchanged(flat, lambda i: i + 2 if i % 2 else i - 2)
    mate = exchanged(flat, lambda i: i ^ 1)
    cross = exchanged(flat, lambda i: i + 1 if i % 2 else i - 1)
    far = exchanged(far, lambda i: i - 2 if i % 2 else i + 2)
    deep_x, both_x, back_y, deep_y, both_y = call(
        second_kernel,
        (
            struct(half_cols, half_cols), struct(half_cols, cols), struct(rows, rows + EDGE),
            struct(planes * rows, planes * rows), struct(planes * rows, planes * rows),
        ), 0, [VMEM],
    )(x_matrix)
    parcel = call(
        depth_kernel, struct(planes // 2 * lo_rows + 2 * count, half_cols), 2, [VMEM] * 4,
        [scratch(planes // 2 * lo_rows, half_cols)],
    )(flags, thresholds, flat, mate, level, deep_x)

    spot = place + jnp.arange(-5, 4)
    owner = (spot + 2 * (spot % 2)) % n
    if full:
        pairs = n // 2
        column = [parcel]
        for q in range(1, pairs):
            column.append(exchanged(parcel, lambda i: i ^ 2 * q))
        column = jnp.stack(column)
        swapped = exchanged(column, lambda i: i ^ 1)
        side = jnp.concatenate([column, swapped])
        index = ((owner % 2) ^ inside) * pairs + ((owner // 2) ^ (place // 2))
    else:
        side = jnp.stack([parcel if o == 0 else shifted(parcel, "gz", -o) for o in range(-5, 6)])
        index = spot + 2 * (spot % 2) - place + 5
    parcels = jnp.stack([side, shifted(side, "gy", 1)])

    coefs, edge = call(
        stack_kernel, (struct(10, rows, cols), struct(10, EDGE, cols)), 1, [VMEM] * 5
    )(flags, flat, mate, level, cross, far)
    edge = shifted(edge, "gy", 1)
    detail = call(
        detail_kernel, struct(count, planes, rows, cols), 1, [VMEM] * 4,
        [scratch(count * planes, rows + EDGE, cols), scratch(count * planes * rows, cols)],
        flops=20_000_000,
    )(thresholds, coefs, edge, back_y, x_matrix)

    kappas = n if full else 6
    cells = float(planes * rows * cols * n * 2)
    denoised, score = call(
        functools.partial(final_kernel, full, cells),
        (struct(planes, count, rows, cols), struct(count if full else 2 * count)), 2, [VMEM] * 5,
        [
            scratch(2 * kappas * rows, half_cols),
            scratch(2 * kappas * rows, half_cols),
            scratch(planes * count * rows, half_cols),
        ],
        score=True,
    )(index.astype(jnp.int32), thresholds, parcels, detail, deep_y, both_y, both_x)
    if not full:
        total = lax.psum(score, ("gz", "gy"))
        score = cells * total[count:] / (total[:count] * total[:count])
    return denoised, score


def solution(mesh):
    in_specs = (P(("cube", "gz"), "gy", None), P())
    out_specs = (P(("cube", "gz"), None, "gy", None), P("cube"))
    return jax.shard_map(body, mesh=mesh, in_specs=in_specs, out_specs=out_specs, check_vma=False)
```

time: 41.8 us -> 36.2 us (0.87)
  starting transfers between devices: 16.5 us -> 12.7 us
  waiting for transfers between devices: 17.1 us -> 14.1 us
  Pallas kernels: 6.32 us -> 7.48 us
    ppermute x9 -> x3, starting transfers between devices: 14.7 us -> 1.15 us  [shifted(): lax.ppermute(array, axis, [(i, (i + by) % devices) for i in range(devices)])]
    ppermute x9 -> x3, waiting for transfers between devices: 14.3 us -> 0.9 us  [shifted(): lax.ppermute(array, axis, [(i, (i + by) % devices) for i in range(devices)])]
    ppermute x1 -> x8, waiting for transfers between devices: 2.77 us -> 13.2 us  [exchanged(): lax.ppermute(array, 'gz', [(i, partner(i) % devices) for i in range(devic...]
    ppermute x1 -> x8, starting transfers between devices: 1.72 us -> 11.6 us  [exchanged(): lax.ppermute(array, 'gz', [(i, partner(i) % devices) for i in range(devic...]
    pallas_call x3 -> x7, Pallas kernels: 6.32 us -> 7.48 us  [run(): pl.pallas_call(kernel, out_shape=out_shape, in_specs=[SMEM] * smem + vmem...]
    slice x1 -> x0, local copies, waits for them, and re-layouts: 0.88 us -> none  [body(): behind = shifted(noisy_cube[:2], 'gz', -1)]
    unnamed x24 -> x8, local copies, waits for them, and re-layouts: 0.07 us -> 0.93 us
  transfers between devices with their start and end apart: 10 -> 11, of which waited for: 6 -> 5; matrix products, arithmetic and copies ran while one was open for 2% -> 0% of each run, Pallas kernels for 0% -> 11%
where the time goes in v1:
time: 36.2 us; the launch traced here: 36.1 us
  waiting for transfers between devices  14.1 us (39%)
  starting transfers between devices  12.7 us (35%)
  Pallas kernels  7.48 us (21%)
  local copies, waits for them, and re-layouts  0.93 us (3%)
  between operations  0.82 us (2%)
    ppermute x8, waiting for transfers between devices, exchanged(): lax.ppermute(array, 'gz', [(i, partner(i) % devices) for i in range(devic...  13.2 us
    ppermute x8, starting transfers between devices, exchanged(): lax.ppermute(array, 'gz', [(i, partner(i) % devices) for i in range(devic...  11.6 us
    pallas_call x7, Pallas kernels, run(): pl.pallas_call(kernel, out_shape=out_shape, in_specs=[SMEM] * smem + vmem...  7.48 us
    ppermute x3, starting transfers between devices, shifted(): lax.ppermute(array, axis, [(i, (i + by) % devices) for i in range(devices)])  1.15 us
    unnamed x8, local copies, waits for them, and re-layouts  0.93 us
    ppermute x3, waiting for transfers between devices, shifted(): lax.ppermute(array, axis, [(i, (i + by) % devices) for i in range(devices)])  0.9 us
  transfers between devices with their start and end apart: 11, of which 5 were waited for; matrix products, arithmetic and copies ran while one was open for 0% of the time, Pallas kernels for 11%

profile of v1, /device:TPU:0, one launch (start us, length us, event | category | flops | bytes accessed | tf_op | source)
XLA Modules:
  0.0 36.1 jit_solution(7893880636510980790)
XLA Ops:
  0.6 0.6 %collective-permute-start = (f32[4,32,256]{2,1,0:T(8,128)}, f32[4,32,256]{2,1,0:T(8,128)S(1)}, u32[]{:S(2)}, u32[]{:S(2)}) collective-permute-start(f32[4,32,256]{2,1,0:T(8,128)} %cube_ref.1), channel_id=1, source_target_pairs={{0,1},{1,0},{2,3},{3,2},{4,5},{5,4},{6,7},{7,6},{8,9},{9,8},{10,11... | collective-permute-start | bytes 393224 | tf_op jit(solution)/shard_map/ppermute | solution.py:325
  1.2 0.0 copy-start
  1.2 0.9 %copy-done = f32[4,32,256]{2,1,0:T(8,128)S(1)} copy-done((f32[4,32,256]{2,1,0:T(8,128)S(1)}, f32[4,32,256]{2,1,0:T(8,128)}, u32[]{:S(2)}) %copy-start) | copy-done | bytes 131096
  2.1 0.3 shard_map.41
  2.4 0.0 collective-permute-done.other_ref
  2.4 0.5 %shard_map.42 = (f32[4,32,256]{2,1,0:T(8,128)S(1)}, f32[2,32,256]{2,1,0:T(8,128)S(1)}) custom-call(s32[1]{0:T(128)} %bitcast.flags_ref, f32[4,32,256]{2,1,0:T(8,128)S(1)} %get-tuple-element.14.own_ref, f32[4,32,256]{2,1,0:T(8,128)S(1)} %collective-permute-done.other_ref, f32[32,64]{1,0:T(8,128)S(1)} %get-tuple-element.15.y_ref, ...), custom_call_target="tpu_custom_call" | custom-call | flops 100000 | tf_op jit(solution)/shard_map/pallas_call | solution.py:352
  3.0 2.8 %collective-permute-start.1 = (f32[4,32,256]{2,1,0:T(8,128)S(1)}, f32[4,32,256]{2,1,0:T(8,128)S(1)}, u32[]{:S(2)}, u32[]{:S(2)}) collective-permute-start(f32[4,32,256]{2,1,0:T(8,128)S(1)} %get-tuple-element.17.own_ref), channel_id=1, source_target_pairs={{0,2},{2,0},{4,6},{6,4},{8,10},{10,8},{12,14},{14,12},{1,3},{3,1},... | collective-permute-start | bytes 393224 | tf_op jit(solution)/shard_map/ppermute | solution.py:330
  5.8 3.6 %collective-permute-start.2 = (f32[4,32,256]{2,1,0:T(8,128)S(1)}, f32[4,32,256]{2,1,0:T(8,128)S(1)}, u32[]{:S(2)}, u32[]{:S(2)}) collective-permute-start(f32[4,32,256]{2,1,0:T(8,128)S(1)} %get-tuple-element.17.own_ref), channel_id=1, source_target_pairs={{0,12},{2,6},{4,0},{6,10},{8,4},{10,14},{12,8},{14,2},{1,13},{3,7}... | collective-permute-start | bytes 393224 | tf_op jit(solution)/shard_map/ppermute | solution.py:330
  9.4 0.5 %shard_map.43 = (f32[128,128]{1,0:T(8,128)S(1)}, f32[128,256]{1,0:T(8,128)S(1)}, f32[32,40]{1,0:T(8,128)S(1)}, f32[128,128]{1,0:T(8,128)S(1)}, f32[128,128]{1,0:T(8,128)S(1)}) custom-call(f32[256,256]{1,0:T(8,128)S(1)} %get-tuple-element.16.x_ref), custom_call_target="tpu_custom_call" | custom-call | flops 100000 | tf_op jit(solution)/shard_map/pallas_call | solution.py:352
  10.0 0.1 collective-permute-start.8
  10.1 0.0 copy-start.1
  10.1 0.1 collective-permute-start.9
  10.1 0.0 collective-permute-done.1.mate_ref
  10.1 3.2 %collective-permute-done.2.level_ref = f32[4,32,256]{2,1,0:T(8,128)S(1)} collective-permute-done((f32[4,32,256]{2,1,0:T(8,128)S(1)}, f32[4,32,256]{2,1,0:T(8,128)S(1)}, u32[]{:S(2)}, u32[]{:S(2)}) %collective-permute-start.2) | collective-permute-done | bytes 131104 | tf_op jit(solution)/shard_map/ppermute | solution.py:330
  13.3 0.0 copy-done.1
  13.3 0.8 %shard_map.44 = f32[40,128]{1,0:T(8,128)S(1)} custom-call(s32[1]{0:T(128)} %bitcast.flags_ref, f32[4]{0:T(128)S(1)} %copy-done.1, f32[4,32,256]{2,1,0:T(8,128)S(1)} %get-tuple-element.17.own_ref, f32[4,32,256]{2,1,0:T(8,128)S(1)} %collective-permute-done.1.mate_ref, f32[4,32,256]{2,1,0:T(8,128)S(1)} %collective-permute-done.2.level_ref, ...), custom_call_target="tpu_custom_call" | custom-call | flops 100000 | tf_op jit(solution)/shard_map/pallas_call | solution.py:352
  14.2 0.3 collective-permute-start.3
  14.5 4.6 %collective-permute-start.4 = (f32[40,128]{1,0:T(8,128)S(1)}, f32[40,128]{1,0:T(8,128)S(1)}, u32[]{:S(2)}, u32[]{:S(2)}) collective-permute-start(f32[40,128]{1,0:T(8,128)S(1)} %shard_map.44), channel_id=1, source_target_pairs={{0,8},{2,10},{4,12},{6,14},{8,0},{10,2},{12,4},{14,6},{1,9},{3,11}... | collective-permute-start | bytes 61448 | tf_op jit(solution)/shard_map/ppermute | solution.py:330
  19.1 0.0 collective-permute-start.5
  19.1 0.0 collective-permute-done.3
  19.1 1.7 %collective-permute-done.4 = f32[40,128]{1,0:T(8,128)S(1)} collective-permute-done((f32[40,128]{1,0:T(8,128)S(1)}, f32[40,128]{1,0:T(8,128)S(1)}, u32[]{:S(2)}, u32[]{:S(2)}) %collective-permute-start.4) | collective-permute-done | bytes 20512 | tf_op jit(solution)/shard_map/ppermute | solution.py:330
  20.9 3.8 %collective-permute-done.5 = f32[40,128]{1,0:T(8,128)S(1)} collective-permute-done((f32[40,128]{1,0:T(8,128)S(1)}, f32[40,128]{1,0:T(8,128)S(1)}, u32[]{:S(2)}, u32[]{:S(2)}) %collective-permute-start.5) | collective-permute-done | bytes 20512 | tf_op jit(solution)/shard_map/ppermute | solution.py:330
  24.7 0.1 collective-permute-start.6
  24.8 4.4 %collective-permute-done.6 = f32[4,40,128]{2,1,0:T(8,128)S(1)} collective-permute-done((f32[4,40,128]{2,1,0:T(8,128)S(1)}, f32[4,40,128]{2,1,0:T(8,128)S(1)}, u32[]{:S(2)}, u32[]{:S(2)}) %collective-permute-start.6) | collective-permute-done | bytes 81952 | tf_op jit(solution)/shard_map/ppermute | solution.py:330
  29.2 0.1 collective-permute-start.7
  29.3 0.0 collective-permute-done.9.far_ref
  29.3 0.0 collective-permute-done.8.cross_ref
  29.3 0.2 shard_map.45
  29.5 0.5 %collective-permute-start.10 = (f32[10,8,256]{2,1,0:T(8,128)S(1)}, f32[10,8,256]{2,1,0:T(8,128)S(1)}, u32[]{:S(2)}, u32[]{:S(2)}) collective-permute-start(f32[10,8,256]{2,1,0:T(8,128)S(1)} %get-tuple-element.21), channel_id=1, source_target_pairs={{0,1},{1,0},{2,3},{3,2},{4,5},{5,4},{6,7},{7,6},{8,9},{9,8},{10,11... | collective-permute-start | bytes 245768 | tf_op jit(solution)/shard_map/ppermute | solution.py:325
  30.1 0.9 %collective-permute-done.10.edge_ref = f32[10,8,256]{2,1,0:T(8,128)S(1)} collective-permute-done((f32[10,8,256]{2,1,0:T(8,128)S(1)}, f32[10,8,256]{2,1,0:T(8,128)S(1)}, u32[]{:S(2)}, u32[]{:S(2)}) %collective-permute-start.10) | collective-permute-done | bytes 81952 | tf_op jit(solution)/shard_map/ppermute | solution.py:325
  31.0 1.9 %shard_map.46.detail_ref = f32[4,4,32,256]{3,2,1,0:T(8,128)S(1)} custom-call(f32[4]{0:T(128)S(1)} %copy-done.1, f32[10,32,256]{2,1,0:T(8,128)S(1)} %get-tuple-element.20.coefs_ref, f32[10,8,256]{2,1,0:T(8,128)S(1)} %collective-permute-done.10.edge_ref, f32[32,40]{1,0:T(8,128)S(1)} %get-tuple-element.22.back_y_ref, f32[256,256]{1,0:T(8,128)S(1)} %get-tuple-element.16.x_ref), custom_call_target="tpu_custom_call" | custom-call | flops 20000000 | tf_op jit(solution)/shard_map/pallas_call | solution.py:352
  32.9 0.0 collective-permute-done.7
  32.9 3.1 %shard_map.47 = (f32[4,4,32,256]{3,2,1,0:T(8,128)}, f32[4]{0:T(128)}) custom-call(s32[9]{0:T(128)S(1)} %fusion.4.index_ref, f32[4]{0:T(128)S(1)} %copy-done.1, f32[2,8,40,128]{3,2,1,0:T(8,128)S(1)} %pad_maximum_fusion.parcels_ref, f32[4,4,32,256]{3,2,1,0:T(8,128)S(1)} %shard_map.46.detail_ref, f32[128,128]{1,0:T(8,128)S(1)} %get-tuple-element.23.deep_y_ref, ...), custom_call_target="tpu_custom_call" | custom-call | flops 100000 | tf_op jit(solution)/shard_map/pallas_call | solution.py:352
  (8 shorter events, 0.1 us)
Async XLA Ops:
  0.6 1.8 %collective-permute-start = (f32[4,32,256]{2,1,0:T(8,128)}, f32[4,32,256]{2,1,0:T(8,128)S(1)}, u32[]{:S(2)}, u32[]{:S(2)}) collective-permute-start(f32[4,32,256]{2,1,0:T(8,128)} %cube_ref.1), channel_id=1, source_target_pairs={{0,1},{1,0},{2,3},{3,2},{4,5},{5,4},{6,7},{7,6},{8,9},{9,8},{10,11... | collective-permute-start | bytes 393224 | tf_op jit(solution)/shard_map/ppermute | solution.py:325
  1.2 0.9 %copy-start = (f32[4,32,256]{2,1,0:T(8,128)S(1)}, f32[4,32,256]{2,1,0:T(8,128)}, u32[]{:S(2)}) copy-start(f32[4,32,256]{2,1,0:T(8,128)} %cube_ref.1) | copy-start | bytes 393220
  3.0 7.2 %collective-permute-start.1 = (f32[4,32,256]{2,1,0:T(8,128)S(1)}, f32[4,32,256]{2,1,0:T(8,128)S(1)}, u32[]{:S(2)}, u32[]{:S(2)}) collective-permute-start(f32[4,32,256]{2,1,0:T(8,128)S(1)} %get-tuple-element.17.own_ref), channel_id=1, source_target_pairs={{0,2},{2,0},{4,6},{6,4},{8,10},{10,8},{12,14},{14,12},{1,3},{3,1},... | collective-permute-start | bytes 393224 | tf_op jit(solution)/shard_map/ppermute | solution.py:330
  5.8 7.5 %collective-permute-start.2 = (f32[4,32,256]{2,1,0:T(8,128)S(1)}, f32[4,32,256]{2,1,0:T(8,128)S(1)}, u32[]{:S(2)}, u32[]{:S(2)}) collective-permute-start(f32[4,32,256]{2,1,0:T(8,128)S(1)} %get-tuple-element.17.own_ref), channel_id=1, source_target_pairs={{0,12},{2,6},{4,0},{6,10},{8,4},{10,14},{12,8},{14,2},{1,13},{3,7}... | collective-permute-start | bytes 393224 | tf_op jit(solution)/shard_map/ppermute | solution.py:330
  10.0 19.4 %collective-permute-start.8 = (f32[4,32,256]{2,1,0:T(8,128)S(1)}, f32[4,32,256]{2,1,0:T(8,128)S(1)}, u32[]{:S(2)}, u32[]{:S(2)}) collective-permute-start(f32[4,32,256]{2,1,0:T(8,128)S(1)} %get-tuple-element.17.own_ref), channel_id=1, source_target_pairs={{0,14},{2,4},{4,2},{6,8},{8,6},{10,12},{12,10},{14,0},{1,15},{3,5}... | collective-permute-start | bytes 393224 | tf_op jit(solution)/shard_map/ppermute | solution.py:330
  10.1 3.3 %copy-start.1 = (f32[4]{0:T(128)S(1)}, f32[4]{0:T(128)}, u32[]{:S(2)}) copy-start(f32[4]{0:T(128)} %limits_ref.5) | copy-start | bytes 52
  10.1 19.2 %collective-permute-start.9 = (f32[2,32,256]{2,1,0:T(8,128)S(1)}, f32[2,32,256]{2,1,0:T(8,128)S(1)}, u32[]{:S(2)}, u32[]{:S(2)}) collective-permute-start(f32[2,32,256]{2,1,0:T(8,128)S(1)} %get-tuple-element.19), channel_id=1, source_target_pairs={{0,4},{2,14},{4,8},{6,2},{8,12},{10,6},{12,0},{14,10},{1,5},{3,15}... | collective-permute-start | bytes 196616 | tf_op jit(solution)/shard_map/ppermute | solution.py:330
  14.2 4.9 %collective-permute-start.3 = (f32[40,128]{1,0:T(8,128)S(1)}, f32[40,128]{1,0:T(8,128)S(1)}, u32[]{:S(2)}, u32[]{:S(2)}) collective-permute-start(f32[40,128]{1,0:T(8,128)S(1)} %shard_map.44), channel_id=1, source_target_pairs={{0,4},{2,6},{4,0},{6,2},{8,12},{10,14},{12,8},{14,10},{1,5},{3,7},... | collective-permute-start | bytes 61448 | tf_op jit(solution)/shard_map/ppermute | solution.py:330
  14.5 6.4 %collective-permute-start.4 = (f32[40,128]{1,0:T(8,128)S(1)}, f32[40,128]{1,0:T(8,128)S(1)}, u32[]{:S(2)}, u32[]{:S(2)}) collective-permute-start(f32[40,128]{1,0:T(8,128)S(1)} %shard_map.44), channel_id=1, source_target_pairs={{0,8},{2,10},{4,12},{6,14},{8,0},{10,2},{12,4},{14,6},{1,9},{3,11}... | collective-permute-start | bytes 61448 | tf_op jit(solution)/shard_map/ppermute | solution.py:330
  19.1 5.6 %collective-permute-start.5 = (f32[40,128]{1,0:T(8,128)S(1)}, f32[40,128]{1,0:T(8,128)S(1)}, u32[]{:S(2)}, u32[]{:S(2)}) collective-permute-start(f32[40,128]{1,0:T(8,128)S(1)} %shard_map.44), channel_id=1, source_target_pairs={{0,12},{2,14},{4,8},{6,10},{8,4},{10,6},{12,0},{14,2},{1,13},{3,15... | collective-permute-start | bytes 61448 | tf_op jit(solution)/shard_map/ppermute | solution.py:330
  24.7 4.5 %collective-permute-start.6 = (f32[4,40,128]{2,1,0:T(8,128)S(1)}, f32[4,40,128]{2,1,0:T(8,128)S(1)}, u32[]{:S(2)}, u32[]{:S(2)}) collective-permute-start(f32[4,40,128]{2,1,0:T(8,128)S(1)} %pad_maximum_fusion.1), channel_id=1, source_target_pairs={{0,2},{2,0},{4,6},{6,4},{8,10},{10,8},{12,14},{14,12},{1,3},{3,1},... | collective-permute-start | bytes 245768 | tf_op jit(solution)/shard_map/ppermute | solution.py:330
  29.2 3.7 %collective-permute-start.7 = (f32[8,40,128]{2,1,0:T(8,128)S(1)}, f32[8,40,128]{2,1,0:T(8,128)S(1)}, u32[]{:S(2)}, u32[]{:S(2)}) collective-permute-start(f32[8,40,128]{2,1,0:T(8,128)S(1)} %constant_dynamic-update-slice_fusion), channel_id=1, source_target_pairs={{0,1},{1,0},{2,3},{3,2},{4,5},{5,4},{6,7},{7,6},{8,9},{9,8},{10,11... | collective-permute-start | bytes 491528 | tf_op jit(solution)/shard_map/ppermute | solution.py:325
  29.5 1.4 %collective-permute-start.10 = (f32[10,8,256]{2,1,0:T(8,128)S(1)}, f32[10,8,256]{2,1,0:T(8,128)S(1)}, u32[]{:S(2)}, u32[]{:S(2)}) collective-permute-start(f32[10,8,256]{2,1,0:T(8,128)S(1)} %get-tuple-element.21), channel_id=1, source_target_pairs={{0,1},{1,0},{2,3},{3,2},{4,5},{5,4},{6,7},{7,6},{8,9},{9,8},{10,11... | collective-permute-start | bytes 245768 | tf_op jit(solution)/shard_map/ppermute | solution.py:325

commit v2 on v1

--- a/solution.py
+++ b/solution.py
@@ -54,12 +54,28 @@
     return last - 2 + row % 4
 
 
-def analysis_tiles(ref):
+def analysis_tiles(ref, across=False):
     length = ref.shape[0]
     half = length // 2
     for band in range(2):
-        shape = (half, length)
-        ref[pl.ds(band * half, half), :] = filter_tile(2 * iota(shape, 0), iota(shape, 1), length, band)
+        shape = (length, half) if across else (half, length)
+        value = filter_tile(2 * iota(shape, int(across)), iota(shape, 1 - int(across)), length, band)
+        if across:
+            ref[:, pl.ds(band * half, half)] = value
+        else:
+            ref[pl.ds(band * half, half), :] = value
+
+
+def split(value):
+    high = value.astype(jnp.bfloat16)
+    return high, (value - high.astype(jnp.float32)).astype(jnp.bfloat16)
+
+
+def split_dot(a, b):
+    def part(left, right):
+        return lax.dot_general(left, right, (((1,), (0,)), ((), ())), preferred_element_type=jnp.float32)
+
+    return part(a[0], b[0]) + (part(a[0], b[1]) + part(a[1], b[0]))
 
 
 def blocks(shape, block):
@@ -67,7 +83,7 @@
     return row % block, column % block, row // block == column // block
 
 
-def first_kernel(cube_ref, x_ref, y_ref, cube_out_ref, semaphore):
+def first_kernel(cube_ref, across_ref, y_ref, cube_out_ref, semaphore):
     copy = pltpu.make_async_copy(cube_ref, cube_out_ref, semaphore)
     copy.start()
     rows, length = y_ref.shape
@@ -75,14 +91,16 @@
     for band in range(2):
         shape = (half, length)
         y_ref[pl.ds(band * half, half), :] = filter_tile(2 * iota(shape, 0), iota(shape, 1), length, band)
+    analysis_tiles(across_ref, True)
+    copy.wait()
+
+
+def second_kernel(x_ref, deep_across_ref, both_x_ref, back_y_ref, both_y_ref, deep_x, deep_y):
     analysis_tiles(x_ref)
-    copy.wait()
-
-
-def second_kernel(x_ref, deep_x_ref, both_x_ref, back_y_ref, deep_y_ref, both_y_ref):
-    half_cols = deep_x_ref.shape[0]
-    analysis_tiles(deep_x_ref)
-    both_x_ref[...] = dot(deep_x_ref[...], x_ref[pl.ds(0, half_cols), :])
+    analysis_tiles(deep_across_ref, True)
+    analysis_tiles(deep_x)
+    half_cols = deep_x.shape[0]
+    both_x_ref[0], both_x_ref[1] = split(dot(deep_x[...], x_ref[pl.ds(0, half_cols), :]))
     shape = back_y_ref.shape
     rows = shape[0]
     half = rows // 2
@@ -95,22 +113,22 @@
         value = filter_tile(2 * edge_rows(column - start, -1), sample, 2 * rows, band)
         total = jnp.where((column >= start) & (column < start + 3), value, total)
     back_y_ref[...] = total
-    row, column, mask = blocks(deep_y_ref.shape, rows)
+    row, column, mask = blocks(deep_y.shape, rows)
     first = 2 * jnp.where(row < half, row, row - half)
     lo = filter_tile(first, column, rows, 0)
     hi = filter_tile(first, column, rows, 1)
-    deep_y_ref[...] = jnp.where(mask, jnp.where(row < half, lo, hi), 0.0)
+    deep_y[...] = jnp.where(mask, jnp.where(row < half, lo, hi), 0.0)
     lows = jnp.where(mask, filter_tile(2 * column, row, 2 * rows, 0), 0.0)
-    both_y_ref[...] = dot(lows, deep_y_ref[...], 1)
-
-
-def plane_kernel(flags_ref, own_ref, other_ref, y_ref, x_ref, out_ref, far_ref, mid):
+    both_y_ref[0], both_y_ref[1] = split(dot(lows, deep_y[...], 1))
+
+
+def plane_kernel(place_ref, own_ref, other_ref, y_ref, x_ref, out_ref, far_ref, mid):
     planes, rows, _ = own_ref.shape
     for z in range(planes):
         plane = jnp.concatenate([own_ref[z], other_ref[z]], 0)
         mid[pl.ds(z * rows, rows), :] = dot(y_ref[...], plane)
-    result = dot(mid[...], x_ref[...], 1)
-    odd = flags_ref[0] == 1
+    result = dot(mid[...], x_ref[...])
+    odd = place_ref[0] % 2 == 1
     for z in range(planes):
         out_ref[z] = result[z * rows : (z + 1) * rows]
     for z in range(2):
@@ -136,13 +154,13 @@
     return jnp.concatenate(rows, 0)
 
 
-def depth_kernel(flags_ref, limits_ref, own_ref, mate_ref, level_ref, deep_x_ref, parcel_ref, lows):
+def depth_kernel(place_ref, limits_ref, own_ref, mate_ref, level_ref, deep_across_ref, parcel_ref, lows):
     planes, rows, cols = own_ref.shape
     count = limits_ref.shape[0]
     squares = [limits_ref[t] * limits_ref[t] for t in range(count)]
     half_cols = cols // 2
     lo_rows = rows // 2
-    odd = flags_ref[0] == 1
+    odd = place_ref[0] % 2 == 1
     sums = [[None] * count, [None] * count]
     for r in range(0, rows, 8):
         for c in range(0, cols, half_cols):
@@ -159,14 +177,14 @@
                         lows[pl.ds(k * lo_rows + r, 8), :] = value
                     else:
                         tally(value, squares, sums)
-    parcel_ref[pl.ds(0, planes // 2 * lo_rows), :] = dot(lows[...], deep_x_ref[...], 1)
+    parcel_ref[pl.ds(0, planes // 2 * lo_rows), :] = dot(lows[...], deep_across_ref[...])
     parcel_ref[pl.ds(planes // 2 * lo_rows, 2 * count), :] = fold(sums)
 
 
-def stack_kernel(flags_ref, own_ref, mate_ref, level_ref, cross_ref, far_ref, out_ref, edge_ref):
+def stack_kernel(place_ref, own_ref, mate_ref, level_ref, cross_ref, far_ref, out_ref, edge_ref):
     planes, rows, cols = own_ref.shape
     half_cols = cols // 2
-    odd = flags_ref[0] == 1
+    odd = place_ref[0] % 2 == 1
     for r in range(0, rows, 8):
         for c in range(0, cols, half_cols):
             at = (pl.ds(r, 8), pl.ds(c, half_cols))
@@ -239,8 +257,8 @@
 
 
 def final_kernel(
-    full, cells, index_ref, limits_ref, parcels_ref, detail_ref, deep_y_ref, both_y_ref, both_x_ref,
-    out_ref, score_ref, zed, mix, coarse,
+    full, cells, place_ref, limits_ref, parcels_ref, detail_ref, both_y_ref, both_x_ref,
+    out_ref, score_ref, zed, mix, coarse, staged, semaphores,
 ):
     count, planes, rows, cols = detail_ref.shape
     half_cols = cols // 2
@@ -251,26 +269,41 @@
     deep_rows = 2 * lo_rows
     pieces = parcels_ref.shape[1]
     kappas = list(range(-5, -5 + pieces)) if full else list(range(-5, 1))
-
-    def place(kap, tap):
+    here = place_ref[0]
+
+    def piece(spot):
+        spot = here + pieces + spot
+        if not full:
+            return spot + 2 * (spot % 2) - here - pieces + 5
+        owner = (spot + 2 * (spot % 2)) % pieces
+        return ((owner % 2) ^ (here % 2)) * (pieces // 2) + ((owner // 2) ^ (here // 2))
+
+    def reach(kap, tap):
         r = 2 * kap + 10 + tap
         return r % (depth * pieces) if full else r
 
+    used = sorted({reach(kap, tap) for kap in kappas for tap in range(8)})
+    spots = {r // depth: piece(r // depth - 5) for r in used}
     for side in range(2):
         for i in range(0, lo_rows, 8):
-            tile = {}
-            for r in sorted({place(kap, tap) for kap in kappas for tap in range(8)}):
-                tile[r] = parcels_ref[side, index_ref[r // depth], pl.ds((r % depth) * lo_rows + i, 8), :]
+            tile = {r: parcels_ref[side, spots[r // depth], pl.ds((r % depth) * lo_rows + i, 8), :] for r in used}
             for a, kap in enumerate(kappas):
                 for band in range(2):
-                    zed[pl.ds((2 * a + band) * deep_rows + side * lo_rows + i, 8), :] = weighted(
-                        (FILTERS[band][tap], tile[place(kap, tap)]) for tap in range(8)
-                    )
-    block = deep_y_ref.shape[0]
-    for a in range(0, zed.shape[0], block):
-        mix[pl.ds(a, block), :] = dot(deep_y_ref[...], zed[pl.ds(a, block), :])
+                    value = weighted((FILTERS[band][tap], tile[reach(kap, tap)]) for tap in range(8))
+                    zed[2 * a + band, pl.ds(side * lo_rows + i, 8), :] = value
+                    if side == 0 and i == 0:
+                        zed[2 * a + band, pl.ds(deep_rows, 8), :] = value
+    for a in range(2 * len(kappas)):
+        for i in range(0, lo_rows, 8):
+            tile = [zed[a, pl.ds(2 * i + tap, 8, stride=2), :] for tap in range(8)]
+            for band in range(2):
+                mix[pl.ds(a * deep_rows + band * lo_rows + i, 8), :] = weighted(zip(FILTERS[band], tile))
 
     low_lanes = iota((8, half_cols), 1) < half_cols // 2
+    block = planes * rows
+    both_y = (both_y_ref[0], both_y_ref[1])
+    both_x = (both_x_ref[0], both_x_ref[1])
+    copies = []
     for t in range(count):
         for i in range(0, deep_rows, 8):
             shrunk = {}
@@ -287,10 +320,12 @@
                 coarse[pl.ds((t * planes + z) * rows + i, 8), :] = weighted(
                     (weight, shrunk[at]) for at, weight in way_back(z).items()
                 )
-        result = dot(both_y_ref[...], coarse[pl.ds(t * block, block), :])
-        result = dot(result, both_x_ref[...])
+        result = split_dot(both_y, split(coarse[pl.ds(t * block, block), :]))
+        result = split_dot(split(result), both_x)
         for z in range(planes):
-            out_ref[z, t] = detail_ref[t, z] + result[z * rows : (z + 1) * rows]
+            staged[t, z] = detail_ref[t, z] + result[z * rows : (z + 1) * rows]
+        copies.append(pltpu.make_async_copy(staged.at[t], out_ref.at[:, t], semaphores.at[t]))
+        copies[-1].start()
 
     sums = [[None] * count, [None] * count]
     for a, kap in enumerate(kappas):
@@ -306,18 +341,20 @@
     total = fold(sums)
     if full:
         for side in range(2):
-            for piece in range(pieces):
-                total = total + parcels_ref[side, piece, pl.ds(depth * lo_rows, 2 * count), :]
+            for at in range(pieces):
+                total = total + parcels_ref[side, at, pl.ds(depth * lo_rows, 2 * count), :]
     else:
         total = total + parcels_ref[0, 5, pl.ds(depth * lo_rows, 2 * count), :]
     for t in range(count):
-        weight = jnp.sum(total[t : t + 1]) * squares[t]
+        weight = jnp.sum(total[t : t + 1] * squares[t][:1])
         residual = jnp.sum(total[count + t : count + t + 1])
         if full:
             score_ref[t] = cells * residual / (weight * weight)
         else:
             score_ref[t] = weight
             score_ref[count + t] = residual
+    for copy in copies:
+        copy.wait()
 
 
 def shifted(array, axis, by):
@@ -346,7 +383,7 @@
 def call(kernel, out_shape, smem, vmem, scratches=(), score=False, flops=100_000):
     out_specs = jax.tree.map(lambda _: VMEM, out_shape)
     if score:
-        out_specs = (VMEM, SMEM)
+        out_specs = (pl.BlockSpec(memory_space=pltpu.HBM), SMEM)
 
     def run(*operands):
         return pl.pallas_call(
@@ -373,11 +410,11 @@
     full = n <= 8 and n & (n - 1) == 0
 
     place = lax.axis_index("gz")
-    inside = place % 2
-    flags = inside.astype(jnp.int32)[None]
+    limits = jnp.broadcast_to(thresholds[:, None, None], (count, 8, half_cols))
+    where = place.astype(jnp.int32)[None]
 
     other = shifted(noisy_cube, "gy", 1)
-    x_matrix, y_matrix, cube = call(
+    across, y_matrix, cube = call(
         first_kernel,
         (
             struct(cols, cols), struct(rows, 2 * rows), struct(planes, rows, cols),
@@ -386,26 +423,26 @@
     flat, far = call(
         plane_kernel, (struct(planes, rows, cols), struct(2, rows, cols)), 1, [VMEM] * 4,
         [scratch(planes * rows, cols)],
-    )(flags, cube, other, y_matrix, x_matrix)
+    )(where, cube, other, y_matrix, across)
 
     level = exchanged(flat, lambda i: i + 2 if i % 2 else i - 2)
     mate = exchanged(flat, lambda i: i ^ 1)
     cross = exchanged(flat, lambda i: i + 1 if i % 2 else i - 1)
     far = exchanged(far, lambda i: i - 2 if i % 2 else i + 2)
-    deep_x, both_x, back_y, deep_y, both_y = call(
+    half = functools.partial(jax.ShapeDtypeStruct, dtype=jnp.bfloat16)
+    block = planes * rows
+    x_matrix, deep_across, both_x, back_y, both_y = call(
         second_kernel,
         (
-            struct(half_cols, half_cols), struct(half_cols, cols), struct(rows, rows + EDGE),
-            struct(planes * rows, planes * rows), struct(planes * rows, planes * rows),
-        ), 0, [VMEM],
-    )(x_matrix)
+            struct(cols, cols), struct(half_cols, half_cols), half((2, half_cols, cols)),
+            struct(rows, rows + EDGE), half((2, block, block)),
+        ), 0, [], [scratch(half_cols, half_cols), scratch(block, block)],
+    )()
     parcel = call(
-        depth_kernel, struct(planes // 2 * lo_rows + 2 * count, half_cols), 2, [VMEM] * 4,
+        depth_kernel, struct(planes // 2 * lo_rows + 2 * count, half_cols), 1, [VMEM] * 5,
         [scratch(planes // 2 * lo_rows, half_cols)],
-    )(flags, thresholds, flat, mate, level, deep_x)
-
-    spot = place + jnp.arange(-5, 4)
-    owner = (spot + 2 * (spot % 2)) % n
+    )(where, limits, flat, mate, level, deep_across)
+
     if full:
         pairs = n // 2
         column = [parcel]
@@ -414,34 +451,34 @@
         column = jnp.stack(column)
         swapped = exchanged(column, lambda i: i ^ 1)
         side = jnp.concatenate([column, swapped])
-        index = ((owner % 2) ^ inside) * pairs + ((owner // 2) ^ (place // 2))
     else:
         side = jnp.stack([parcel if o == 0 else shifted(parcel, "gz", -o) for o in range(-5, 6)])
-        index = spot + 2 * (spot % 2) - place + 5
     parcels = jnp.stack([side, shifted(side, "gy", 1)])
 
     coefs, edge = call(
         stack_kernel, (struct(10, rows, cols), struct(10, EDGE, cols)), 1, [VMEM] * 5
-    )(flags, flat, mate, level, cross, far)
+    )(where, flat, mate, level, cross, far)
     edge = shifted(edge, "gy", 1)
     detail = call(
-        detail_kernel, struct(count, planes, rows, cols), 1, [VMEM] * 4,
+        detail_kernel, struct(count, planes, rows, cols), 0, [VMEM] * 5,
         [scratch(count * planes, rows + EDGE, cols), scratch(count * planes * rows, cols)],
         flops=20_000_000,
-    )(thresholds, coefs, edge, back_y, x_matrix)
+    )(limits, coefs, edge, back_y, x_matrix)
 
     kappas = n if full else 6
     cells = float(planes * rows * cols * n * 2)
     denoised, score = call(
         functools.partial(final_kernel, full, cells),
-        (struct(planes, count, rows, cols), struct(count if full else 2 * count)), 2, [VMEM] * 5,
+        (struct(planes, count, rows, cols), struct(count if full else 2 * count)), 1, [VMEM] * 5,
         [
+            scratch(2 * kappas, rows + EDGE, half_cols),
             scratch(2 * kappas * rows, half_cols),
-            scratch(2 * kappas * rows, half_cols),
-            scratch(planes * count * rows, half_cols),
+            scratch(count * block, half_cols),
+            scratch(count, planes, rows, cols),
+            pltpu.SemaphoreType.DMA((count,)),
         ],
         score=True,
-    )(index.astype(jnp.int32), thresholds, parcels, detail, deep_y, both_y, both_x)
+    )(where, limits, parcels, detail, both_y, both_x)
     if not full:
         total = lax.psum(score, ("gz", "gy"))
         score = cells * total[count:] / (total[:count] * total[:count])

time: 36.2 us -> 37.6 us (1.039)
  Pallas kernels: 7.48 us -> 5.76 us
  starting transfers between devices: 12.7 us -> 14.4 us
  waiting for transfers between devices: 14.1 us -> 15.5 us
    ppermute x8, starting transfers between devices: 11.6 us -> 13.7 us  [exchanged(): lax.ppermute(array, 'gz', [(i, partner(i) % devices) for i in range(devic...]
    pallas_call x7, Pallas kernels: 7.48 us -> 5.76 us  [run(): pl.pallas_call(kernel, out_shape=out_shape, in_specs=[SMEM] * smem + vmem...]
    ppermute x8, waiting for transfers between devices: 13.2 us -> 14.3 us  [exchanged(): lax.ppermute(array, 'gz', [(i, partner(i) % devices) for i in range(devic...]
    ppermute x3, starting transfers between devices: 1.15 us -> 0.7 us  [shifted(): lax.ppermute(array, axis, [(i, (i + by) % devices) for i in range(devices)])]
  transfers between devices with their start and end apart: 11 -> 11, of which waited for: 5 -> 7; matrix products, arithmetic and copies ran while one was open for 0% -> 0% of each run, Pallas kernels for 11% -> 7%
where the time goes in v2:
time: 37.6 us; the launch traced here: 37.5 us
  waiting for transfers between devices  15.5 us (41%)
  starting transfers between devices  14.4 us (38%)
  Pallas kernels  5.76 us (15%)
  local copies, waits for them, and re-layouts  1 us (3%)
  between operations  0.73 us (2%)
    ppermute x8, waiting for transfers between devices, exchanged(): lax.ppermute(array, 'gz', [(i, partner(i) % devices) for i in range(devic...  14.3 us
    ppermute x8, starting transfers between devices, exchanged(): lax.ppermute(array, 'gz', [(i, partner(i) % devices) for i in range(devic...  13.7 us
    pallas_call x7, Pallas kernels, run(): pl.pallas_call(kernel, out_shape=out_shape, in_specs=[SMEM] * smem + vmem...  5.76 us
    ppermute x3, waiting for transfers between devices, shifted(): lax.ppermute(array, axis, [(i, (i + by) % devices) for i in range(devices)])  1.27 us
    unnamed x8, local copies, waits for them, and re-layouts  0.92 us
  transfers between devices with their start and end apart: 11, of which 7 were waited for; matrix products, arithmetic and copies ran while one was open for 0% of the time, Pallas kernels for 7%

profile of v2, /device:TPU:0, one launch (start us, length us, event | category | flops | bytes accessed | tf_op | source)
XLA Modules:
  0.0 37.5 jit_solution(6035506464128835461)
XLA Ops:
  0.6 0.6 %collective-permute-start = (f32[4,32,256]{2,1,0:T(8,128)}, f32[4,32,256]{2,1,0:T(8,128)S(1)}, u32[]{:S(2)}, u32[]{:S(2)}) collective-permute-start(f32[4,32,256]{2,1,0:T(8,128)} %cube_ref.1), channel_id=1, source_target_pairs={{0,1},{1,0},{2,3},{3,2},{4,5},{5,4},{6,7},{7,6},{8,9},{9,8},{10,11... | collective-permute-start | bytes 393224 | tf_op jit(solution)/shard_map/ppermute | solution.py:362
  1.2 0.0 copy-start
  1.2 0.9 %copy-done = f32[4,32,256]{2,1,0:T(8,128)S(1)} copy-done((f32[4,32,256]{2,1,0:T(8,128)S(1)}, f32[4,32,256]{2,1,0:T(8,128)}, u32[]{:S(2)}) %copy-start) | copy-done | bytes 131096
  2.1 0.3 shard_map.41
  2.4 0.0 collective-permute-done.other_ref
  2.4 0.5 %shard_map.42 = (f32[4,32,256]{2,1,0:T(8,128)S(1)}, f32[2,32,256]{2,1,0:T(8,128)S(1)}) custom-call(s32[1]{0:T(128)} %bitcast.place_ref, f32[4,32,256]{2,1,0:T(8,128)S(1)} %get-tuple-element.14.own_ref, f32[4,32,256]{2,1,0:T(8,128)S(1)} %collective-permute-done.other_ref, f32[32,64]{1,0:T(8,128)S(1)} %get-tuple-element.15.y_ref, ...), custom_call_target="tpu_custom_call" | custom-call | flops 100000 | tf_op jit(solution)/shard_map/pallas_call | solution.py:389
  2.9 0.0 copy-start.1
  2.9 5.0 %collective-permute-start.2 = (f32[4,32,256]{2,1,0:T(8,128)S(1)}, f32[4,32,256]{2,1,0:T(8,128)S(1)}, u32[]{:S(2)}, u32[]{:S(2)}) collective-permute-start(f32[4,32,256]{2,1,0:T(8,128)S(1)} %get-tuple-element.17.own_ref), channel_id=1, source_target_pairs={{0,12},{2,6},{4,0},{6,10},{8,4},{10,14},{12,8},{14,2},{1,13},{3,7}... | collective-permute-start | bytes 393224 | tf_op jit(solution)/shard_map/ppermute | solution.py:367
  7.9 0.0 collective-permute-start.1
  7.9 0.6 %shard_map.43 = (f32[256,256]{1,0:T(8,128)S(1)}, f32[128,128]{1,0:T(8,128)S(1)}, bf16[2,128,256]{2,1,0:T(8,128)(2,1)S(1)}, f32[32,40]{1,0:T(8,128)S(1)}, bf16[2,128,128]{2,1,0:T(8,128)(2,1)S(1)}) custom-call(), custom_call_target="tpu_custom_call" | custom-call | flops 100000 | tf_op jit(solution)/shard_map/pallas_call | solution.py:389
  8.5 2.0 %collective-permute-start.8 = (f32[4,32,256]{2,1,0:T(8,128)S(1)}, f32[4,32,256]{2,1,0:T(8,128)S(1)}, u32[]{:S(2)}, u32[]{:S(2)}) collective-permute-start(f32[4,32,256]{2,1,0:T(8,128)S(1)} %get-tuple-element.17.own_ref), channel_id=1, source_target_pairs={{0,14},{2,4},{4,2},{6,8},{8,6},{10,12},{12,10},{14,0},{1,15},{3,5}... | collective-permute-start | bytes 393224 | tf_op jit(solution)/shard_map/ppermute | solution.py:367
  10.5 1.2 %collective-permute-done.2.level_ref = f32[4,32,256]{2,1,0:T(8,128)S(1)} collective-permute-done((f32[4,32,256]{2,1,0:T(8,128)S(1)}, f32[4,32,256]{2,1,0:T(8,128)S(1)}, u32[]{:S(2)}, u32[]{:S(2)}) %collective-permute-start.2) | collective-permute-done | bytes 131104 | tf_op jit(solution)/shard_map/ppermute | solution.py:367
  11.7 1.5 %collective-permute-done.1.mate_ref = f32[4,32,256]{2,1,0:T(8,128)S(1)} collective-permute-done((f32[4,32,256]{2,1,0:T(8,128)S(1)}, f32[4,32,256]{2,1,0:T(8,128)S(1)}, u32[]{:S(2)}, u32[]{:S(2)}) %collective-permute-start.1) | collective-permute-done | bytes 131104 | tf_op jit(solution)/shard_map/ppermute | solution.py:367
  13.2 0.0 copy-done.1
  13.2 0.1 broadcast_in_dim.10.limits_ref
  13.3 0.2 shard_map.44
  13.5 2.9 %collective-permute-start.5 = (f32[40,128]{1,0:T(8,128)S(1)}, f32[40,128]{1,0:T(8,128)S(1)}, u32[]{:S(2)}, u32[]{:S(2)}) collective-permute-start(f32[40,128]{1,0:T(8,128)S(1)} %shard_map.44), channel_id=1, source_target_pairs={{0,12},{2,14},{4,8},{6,10},{8,4},{10,6},{12,0},{14,2},{1,13},{3,15... | collective-permute-start | bytes 61448 | tf_op jit(solution)/shard_map/ppermute | solution.py:367
  16.4 0.0 collective-permute-start.4
  16.4 1.6 %collective-permute-start.3 = (f32[40,128]{1,0:T(8,128)S(1)}, f32[40,128]{1,0:T(8,128)S(1)}, u32[]{:S(2)}, u32[]{:S(2)}) collective-permute-start(f32[40,128]{1,0:T(8,128)S(1)} %shard_map.44), channel_id=1, source_target_pairs={{0,4},{2,6},{4,0},{6,2},{8,12},{10,14},{12,8},{14,10},{1,5},{3,7},... | collective-permute-start | bytes 61448 | tf_op jit(solution)/shard_map/ppermute | solution.py:367
  17.9 1.2 %collective-permute-done.5 = f32[40,128]{1,0:T(8,128)S(1)} collective-permute-done((f32[40,128]{1,0:T(8,128)S(1)}, f32[40,128]{1,0:T(8,128)S(1)}, u32[]{:S(2)}, u32[]{:S(2)}) %collective-permute-start.5) | collective-permute-done | bytes 20512 | tf_op jit(solution)/shard_map/ppermute | solution.py:367
  19.1 1.9 %collective-permute-done.4 = f32[40,128]{1,0:T(8,128)S(1)} collective-permute-done((f32[40,128]{1,0:T(8,128)S(1)}, f32[40,128]{1,0:T(8,128)S(1)}, u32[]{:S(2)}, u32[]{:S(2)}) %collective-permute-start.4) | collective-permute-done | bytes 20512 | tf_op jit(solution)/shard_map/ppermute | solution.py:367
  21.1 0.0 collective-permute-done.3
  21.1 1.6 %collective-permute-start.6 = (f32[4,40,128]{2,1,0:T(8,128)S(1)}, f32[4,40,128]{2,1,0:T(8,128)S(1)}, u32[]{:S(2)}, u32[]{:S(2)}) collective-permute-start(f32[4,40,128]{2,1,0:T(8,128)S(1)} %pad_maximum_fusion.1), channel_id=1, source_target_pairs={{0,2},{2,0},{4,6},{6,4},{8,10},{10,8},{12,14},{14,12},{1,3},{3,1},... | collective-permute-start | bytes 245768 | tf_op jit(solution)/shard_map/ppermute | solution.py:367
  22.7 2.9 %collective-permute-done.6 = f32[4,40,128]{2,1,0:T(8,128)S(1)} collective-permute-done((f32[4,40,128]{2,1,0:T(8,128)S(1)}, f32[4,40,128]{2,1,0:T(8,128)S(1)}, u32[]{:S(2)}, u32[]{:S(2)}) %collective-permute-start.6) | collective-permute-done | bytes 81952 | tf_op jit(solution)/shard_map/ppermute | solution.py:367
  25.6 0.1 collective-permute-start.7
  25.7 0.7 %collective-permute-start.9 = (f32[2,32,256]{2,1,0:T(8,128)S(1)}, f32[2,32,256]{2,1,0:T(8,128)S(1)}, u32[]{:S(2)}, u32[]{:S(2)}) collective-permute-start(f32[2,32,256]{2,1,0:T(8,128)S(1)} %get-tuple-element.19), channel_id=1, source_target_pairs={{0,4},{2,14},{4,8},{6,2},{8,12},{10,6},{12,0},{14,10},{1,5},{3,15}... | collective-permute-start | bytes 196616 | tf_op jit(solution)/shard_map/ppermute | solution.py:367
  26.4 5.6 %collective-permute-done.9.far_ref = f32[2,32,256]{2,1,0:T(8,128)S(1)} collective-permute-done((f32[2,32,256]{2,1,0:T(8,128)S(1)}, f32[2,32,256]{2,1,0:T(8,128)S(1)}, u32[]{:S(2)}, u32[]{:S(2)}) %collective-permute-start.9) | collective-permute-done | bytes 65568 | tf_op jit(solution)/shard_map/ppermute | solution.py:367
  32.0 0.0 collective-permute-done.8.cross_ref
  32.0 0.2 shard_map.45
  32.2 0.1 collective-permute-start.10
  32.2 1.3 %collective-permute-done.10.edge_ref = f32[10,8,256]{2,1,0:T(8,128)S(1)} collective-permute-done((f32[10,8,256]{2,1,0:T(8,128)S(1)}, f32[10,8,256]{2,1,0:T(8,128)S(1)}, u32[]{:S(2)}, u32[]{:S(2)}) %collective-permute-start.10) | collective-permute-done | bytes 81952 | tf_op jit(solution)/shard_map/ppermute | solution.py:362
  33.5 1.4 %shard_map.46.detail_ref = f32[4,4,32,256]{3,2,1,0:T(8,128)S(1)} custom-call(f32[4,8,128]{2,1,0:T(8,128)S(1)} %broadcast_in_dim.10.limits_ref, f32[10,32,256]{2,1,0:T(8,128)S(1)} %get-tuple-element.20.coefs_ref, f32[10,8,256]{2,1,0:T(8,128)S(1)} %collective-permute-done.10.edge_ref, f32[32,40]{1,0:T(8,128)S(1)} %get-tuple-element.22.back_y_ref, ...), custom_call_target="tpu_custom_call" | custom-call | flops 20000000 | tf_op jit(solution)/shard_map/pallas_call | solution.py:389
  34.9 0.0 collective-permute-done.7
  34.9 2.6 %shard_map.47 = (f32[4,4,32,256]{3,2,1,0:T(8,128)}, f32[4]{0:T(128)}) custom-call(s32[1]{0:T(128)} %bitcast.place_ref, f32[4,8,128]{2,1,0:T(8,128)S(1)} %broadcast_in_dim.10.limits_ref, f32[2,8,40,128]{3,2,1,0:T(8,128)S(1)} %pad_maximum_fusion.parcels_ref, f32[4,4,32,256]{3,2,1,0:T(8,128)S(1)} %shard_map.46.detail_ref, ...), custom_call_target="tpu_custom_call" | custom-call | flops 100000 | tf_op jit(solution)/shard_map/pallas_call | solution.py:389
  (7 shorter events, 0.0 us)
Async XLA Ops:
  0.6 1.8 %collective-permute-start = (f32[4,32,256]{2,1,0:T(8,128)}, f32[4,32,256]{2,1,0:T(8,128)S(1)}, u32[]{:S(2)}, u32[]{:S(2)}) collective-permute-start(f32[4,32,256]{2,1,0:T(8,128)} %cube_ref.1), channel_id=1, source_target_pairs={{0,1},{1,0},{2,3},{3,2},{4,5},{5,4},{6,7},{7,6},{8,9},{9,8},{10,11... | collective-permute-start | bytes 393224 | tf_op jit(solution)/shard_map/ppermute | solution.py:362
  1.2 0.9 %copy-start = (f32[4,32,256]{2,1,0:T(8,128)S(1)}, f32[4,32,256]{2,1,0:T(8,128)}, u32[]{:S(2)}) copy-start(f32[4,32,256]{2,1,0:T(8,128)} %cube_ref.1) | copy-start | bytes 393220
  2.9 10.3 %copy-start.1 = (f32[4]{0:T(128)S(1)}, f32[4]{0:T(128)}, u32[]{:S(2)}) copy-start(f32[4]{0:T(128)} %param.3) | copy-start | bytes 52
  2.9 8.8 %collective-permute-start.2 = (f32[4,32,256]{2,1,0:T(8,128)S(1)}, f32[4,32,256]{2,1,0:T(8,128)S(1)}, u32[]{:S(2)}, u32[]{:S(2)}) collective-permute-start(f32[4,32,256]{2,1,0:T(8,128)S(1)} %get-tuple-element.17.own_ref), channel_id=1, source_target_pairs={{0,12},{2,6},{4,0},{6,10},{8,4},{10,14},{12,8},{14,2},{1,13},{3,7}... | collective-permute-start | bytes 393224 | tf_op jit(solution)/shard_map/ppermute | solution.py:367
  7.9 5.3 %collective-permute-start.1 = (f32[4,32,256]{2,1,0:T(8,128)S(1)}, f32[4,32,256]{2,1,0:T(8,128)S(1)}, u32[]{:S(2)}, u32[]{:S(2)}) collective-permute-start(f32[4,32,256]{2,1,0:T(8,128)S(1)} %get-tuple-element.17.own_ref), channel_id=1, source_target_pairs={{0,2},{2,0},{4,6},{6,4},{8,10},{10,8},{12,14},{14,12},{1,3},{3,1},... | collective-permute-start | bytes 393224 | tf_op jit(solution)/shard_map/ppermute | solution.py:367
  8.5 23.4 %collective-permute-start.8 = (f32[4,32,256]{2,1,0:T(8,128)S(1)}, f32[4,32,256]{2,1,0:T(8,128)S(1)}, u32[]{:S(2)}, u32[]{:S(2)}) collective-permute-start(f32[4,32,256]{2,1,0:T(8,128)S(1)} %get-tuple-element.17.own_ref), channel_id=1, source_target_pairs={{0,14},{2,4},{4,2},{6,8},{8,6},{10,12},{12,10},{14,0},{1,15},{3,5}... | collective-permute-start | bytes 393224 | tf_op jit(solution)/shard_map/ppermute | solution.py:367
  13.5 5.6 %collective-permute-start.5 = (f32[40,128]{1,0:T(8,128)S(1)}, f32[40,128]{1,0:T(8,128)S(1)}, u32[]{:S(2)}, u32[]{:S(2)}) collective-permute-start(f32[40,128]{1,0:T(8,128)S(1)} %shard_map.44), channel_id=1, source_target_pairs={{0,12},{2,14},{4,8},{6,10},{8,4},{10,6},{12,0},{14,2},{1,13},{3,15... | collective-permute-start | bytes 61448 | tf_op jit(solution)/shard_map/ppermute | solution.py:367
  16.4 4.7 %collective-permute-start.4 = (f32[40,128]{1,0:T(8,128)S(1)}, f32[40,128]{1,0:T(8,128)S(1)}, u32[]{:S(2)}, u32[]{:S(2)}) collective-permute-start(f32[40,128]{1,0:T(8,128)S(1)} %shard_map.44), channel_id=1, source_target_pairs={{0,8},{2,10},{4,12},{6,14},{8,0},{10,2},{12,4},{14,6},{1,9},{3,11}... | collective-permute-start | bytes 61448 | tf_op jit(solution)/shard_map/ppermute | solution.py:367
  16.4 4.7 %collective-permute-start.3 = (f32[40,128]{1,0:T(8,128)S(1)}, f32[40,128]{1,0:T(8,128)S(1)}, u32[]{:S(2)}, u32[]{:S(2)}) collective-permute-start(f32[40,128]{1,0:T(8,128)S(1)} %shard_map.44), channel_id=1, source_target_pairs={{0,4},{2,6},{4,0},{6,2},{8,12},{10,14},{12,8},{14,10},{1,5},{3,7},... | collective-permute-start | bytes 61448 | tf_op jit(solution)/shard_map/ppermute | solution.py:367
  21.1 4.5 %collective-permute-start.6 = (f32[4,40,128]{2,1,0:T(8,128)S(1)}, f32[4,40,128]{2,1,0:T(8,128)S(1)}, u32[]{:S(2)}, u32[]{:S(2)}) collective-permute-start(f32[4,40,128]{2,1,0:T(8,128)S(1)} %pad_maximum_fusion.1), channel_id=1, source_target_pairs={{0,2},{2,0},{4,6},{6,4},{8,10},{10,8},{12,14},{14,12},{1,3},{3,1},... | collective-permute-start | bytes 245768 | tf_op jit(solution)/shard_map/ppermute | solution.py:367
  25.6 9.3 %collective-permute-start.7 = (f32[8,40,128]{2,1,0:T(8,128)S(1)}, f32[8,40,128]{2,1,0:T(8,128)S(1)}, u32[]{:S(2)}, u32[]{:S(2)}) collective-permute-start(f32[8,40,128]{2,1,0:T(8,128)S(1)} %constant_dynamic-update-slice_fusion), channel_id=1, source_target_pairs={{0,1},{1,0},{2,3},{3,2},{4,5},{5,4},{6,7},{7,6},{8,9},{9,8},{10,11... | collective-permute-start | bytes 491528 | tf_op jit(solution)/shard_map/ppermute | solution.py:362
  25.7 6.3 %collective-permute-start.9 = (f32[2,32,256]{2,1,0:T(8,128)S(1)}, f32[2,32,256]{2,1,0:T(8,128)S(1)}, u32[]{:S(2)}, u32[]{:S(2)}) collective-permute-start(f32[2,32,256]{2,1,0:T(8,128)S(1)} %get-tuple-element.19), channel_id=1, source_target_pairs={{0,4},{2,14},{4,8},{6,2},{8,12},{10,6},{12,0},{14,10},{1,5},{3,15}... | collective-permute-start | bytes 196616 | tf_op jit(solution)/shard_map/ppermute | solution.py:367
  32.2 1.3 %collective-permute-start.10 = (f32[10,8,256]{2,1,0:T(8,128)S(1)}, f32[10,8,256]{2,1,0:T(8,128)S(1)}, u32[]{:S(2)}, u32[]{:S(2)}) collective-permute-start(f32[10,8,256]{2,1,0:T(8,128)S(1)} %get-tuple-element.21), channel_id=1, source_target_pairs={{0,1},{1,0},{2,3},{3,2},{4,5},{5,4},{6,7},{7,6},{8,9},{9,8},{10,11... | collective-permute-start | bytes 245768 | tf_op jit(solution)/shard_map/ppermute | solution.py:362

commit v3 on v2

--- a/solution.py
+++ b/solution.py
@@ -276,7 +276,7 @@
         if not full:
             return spot + 2 * (spot % 2) - here - pieces + 5
         owner = (spot + 2 * (spot % 2)) % pieces
-        return ((owner % 2) ^ (here % 2)) * (pieces // 2) + ((owner // 2) ^ (here // 2))
+        return ((owner // 2) ^ (here // 2)) * 2 + ((owner % 2) ^ (here % 2))
 
     def reach(kap, tap):
         r = 2 * kap + 10 + tap
@@ -427,7 +427,6 @@
 
     level = exchanged(flat, lambda i: i + 2 if i % 2 else i - 2)
     mate = exchanged(flat, lambda i: i ^ 1)
-    cross = exchanged(flat, lambda i: i + 1 if i % 2 else i - 1)
     far = exchanged(far, lambda i: i - 2 if i % 2 else i + 2)
     half = functools.partial(jax.ShapeDtypeStruct, dtype=jnp.bfloat16)
     block = planes * rows
@@ -445,16 +444,16 @@
 
     if full:
         pairs = n // 2
-        column = [parcel]
+        column = jnp.stack([parcel, exchanged(parcel, lambda i: i ^ 1)])
+        side = [column]
         for q in range(1, pairs):
-            column.append(exchanged(parcel, lambda i: i ^ 2 * q))
-        column = jnp.stack(column)
-        swapped = exchanged(column, lambda i: i ^ 1)
-        side = jnp.concatenate([column, swapped])
+            side.append(exchanged(column, lambda i: i ^ 2 * q))
+        side = jnp.concatenate(side)
     else:
         side = jnp.stack([parcel if o == 0 else shifted(parcel, "gz", -o) for o in range(-5, 6)])
     parcels = jnp.stack([side, shifted(side, "gy", 1)])
 
+    cross = exchanged(level, lambda i: i ^ 1)
     coefs, edge = call(
         stack_kernel, (struct(10, rows, cols), struct(10, EDGE, cols)), 1, [VMEM] * 5
     )(where, flat, mate, level, cross, far)

time: 37.6 us -> 36.4 us (0.968)
  starting transfers between devices: 14.4 us -> 13.6 us
  waiting for transfers between devices: 15.5 us -> 15.1 us
    ppermute x8, starting transfers between devices: 13.7 us -> 12.9 us  [exchanged(): lax.ppermute(array, 'gz', [(i, partner(i) % devices) for i in range(devic...]
    ppermute x8, waiting for transfers between devices: 14.3 us -> 13.8 us  [exchanged(): lax.ppermute(array, 'gz', [(i, partner(i) % devices) for i in range(devic...]
where the time goes in v3:
time: 36.4 us; the launch traced here: 36.2 us
  waiting for transfers between devices  15.1 us (41%)
  starting transfers between devices  13.6 us (37%)
  Pallas kernels  5.75 us (16%)
  local copies, waits for them, and re-layouts  1 us (3%)
  between operations  0.74 us (2%)
    ppermute x8, waiting for transfers between devices, exchanged(): lax.ppermute(array, 'gz', [(i, partner(i) % devices) for i in range(devic...  13.8 us
    ppermute x8, starting transfers between devices, exchanged(): lax.ppermute(array, 'gz', [(i, partner(i) % devices) for i in range(devic...  12.9 us
    pallas_call x7, Pallas kernels, run(): pl.pallas_call(kernel, out_shape=out_shape, in_specs=[SMEM] * smem + vmem...  5.75 us
    ppermute x3, waiting for transfers between devices, shifted(): lax.ppermute(array, axis, [(i, (i + by) % devices) for i in range(devices)])  1.27 us
    unnamed x8, local copies, waits for them, and re-layouts  0.92 us
  transfers between devices with their start and end apart: 11, of which 7 were waited for; matrix products, arithmetic and copies ran while one was open for 0% of the time, Pallas kernels for 7%

profile of v3, /device:TPU:0, one launch (start us, length us, event | category | flops | bytes accessed | tf_op | source)
XLA Modules:
  0.0 36.2 jit_solution(726423295352369797)
XLA Ops:
  0.6 0.6 %collective-permute-start = (f32[4,32,256]{2,1,0:T(8,128)}, f32[4,32,256]{2,1,0:T(8,128)S(1)}, u32[]{:S(2)}, u32[]{:S(2)}) collective-permute-start(f32[4,32,256]{2,1,0:T(8,128)} %cube_ref.1), channel_id=1, source_target_pairs={{0,1},{1,0},{2,3},{3,2},{4,5},{5,4},{6,7},{7,6},{8,9},{9,8},{10,11... | collective-permute-start | bytes 393224 | tf_op jit(solution)/shard_map/ppermute | solution.py:362
  1.2 0.0 copy-start
  1.2 0.9 %copy-done = f32[4,32,256]{2,1,0:T(8,128)S(1)} copy-done((f32[4,32,256]{2,1,0:T(8,128)S(1)}, f32[4,32,256]{2,1,0:T(8,128)}, u32[]{:S(2)}) %copy-start) | copy-done | bytes 131096
  2.1 0.3 shard_map.41
  2.4 0.0 collective-permute-done.other_ref
  2.4 0.5 %shard_map.42 = (f32[4,32,256]{2,1,0:T(8,128)S(1)}, f32[2,32,256]{2,1,0:T(8,128)S(1)}) custom-call(s32[1]{0:T(128)} %bitcast.place_ref, f32[4,32,256]{2,1,0:T(8,128)S(1)} %get-tuple-element.14.own_ref, f32[4,32,256]{2,1,0:T(8,128)S(1)} %collective-permute-done.other_ref, f32[32,64]{1,0:T(8,128)S(1)} %get-tuple-element.15.y_ref, ...), custom_call_target="tpu_custom_call" | custom-call | flops 100000 | tf_op jit(solution)/shard_map/pallas_call | solution.py:389
  2.9 0.0 copy-start.1
  2.9 5.0 %collective-permute-start.2 = (f32[4,32,256]{2,1,0:T(8,128)S(1)}, f32[4,32,256]{2,1,0:T(8,128)S(1)}, u32[]{:S(2)}, u32[]{:S(2)}) collective-permute-start(f32[4,32,256]{2,1,0:T(8,128)S(1)} %get-tuple-element.17.own_ref), channel_id=1, source_target_pairs={{0,12},{2,6},{4,0},{6,10},{8,4},{10,14},{12,8},{14,2},{1,13},{3,7}... | collective-permute-start | bytes 393224 | tf_op jit(solution)/shard_map/ppermute | solution.py:367
  7.9 0.0 collective-permute-start.1
  7.9 0.6 %shard_map.43 = (f32[256,256]{1,0:T(8,128)S(1)}, f32[128,128]{1,0:T(8,128)S(1)}, bf16[2,128,256]{2,1,0:T(8,128)(2,1)S(1)}, f32[32,40]{1,0:T(8,128)S(1)}, bf16[2,128,128]{2,1,0:T(8,128)(2,1)S(1)}) custom-call(), custom_call_target="tpu_custom_call" | custom-call | flops 100000 | tf_op jit(solution)/shard_map/pallas_call | solution.py:389
  8.5 2.5 %collective-permute-done.2.level_ref = f32[4,32,256]{2,1,0:T(8,128)S(1)} collective-permute-done((f32[4,32,256]{2,1,0:T(8,128)S(1)}, f32[4,32,256]{2,1,0:T(8,128)S(1)}, u32[]{:S(2)}, u32[]{:S(2)}) %collective-permute-start.2) | collective-permute-done | bytes 131104 | tf_op jit(solution)/shard_map/ppermute | solution.py:367
  11.0 2.2 %collective-permute-done.1.mate_ref = f32[4,32,256]{2,1,0:T(8,128)S(1)} collective-permute-done((f32[4,32,256]{2,1,0:T(8,128)S(1)}, f32[4,32,256]{2,1,0:T(8,128)S(1)}, u32[]{:S(2)}, u32[]{:S(2)}) %collective-permute-start.1) | collective-permute-done | bytes 131104 | tf_op jit(solution)/shard_map/ppermute | solution.py:367
  13.2 0.0 copy-done.1
  13.2 0.1 broadcast_in_dim.10.limits_ref
  13.3 0.2 shard_map.44
  13.5 0.3 collective-permute-start.3
  13.8 1.7 %collective-permute-start.8 = (f32[4,32,256]{2,1,0:T(8,128)S(1)}, f32[4,32,256]{2,1,0:T(8,128)S(1)}, u32[]{:S(2)}, u32[]{:S(2)}) collective-permute-start(f32[4,32,256]{2,1,0:T(8,128)S(1)} %collective-permute-done.2.level_ref), channel_id=1, source_target_pairs={{0,2},{2,0},{4,6},{6,4},{8,10},{10,8},{12,14},{14,12},{1,3},{3,1},... | collective-permute-start | bytes 393224 | tf_op jit(solution)/shard_map/ppermute | solution.py:367
  15.6 1.8 %collective-permute-done.3 = f32[40,128]{1,0:T(8,128)S(1)} collective-permute-done((f32[40,128]{1,0:T(8,128)S(1)}, f32[40,128]{1,0:T(8,128)S(1)}, u32[]{:S(2)}, u32[]{:S(2)}) %collective-permute-start.3) | collective-permute-done | bytes 20512 | tf_op jit(solution)/shard_map/ppermute | solution.py:367
  17.3 2.1 %collective-permute-start.6 = (f32[2,40,128]{2,1,0:T(8,128)S(1)}, f32[2,40,128]{2,1,0:T(8,128)S(1)}, u32[]{:S(2)}, u32[]{:S(2)}) collective-permute-start(f32[2,40,128]{2,1,0:T(8,128)S(1)} %pad_maximum_fusion.1), channel_id=1, source_target_pairs={{0,12},{2,14},{4,8},{6,10},{8,4},{10,6},{12,0},{14,2},{1,13},{3,15... | collective-permute-start | bytes 122888 | tf_op jit(solution)/shard_map/ppermute | solution.py:367
  19.4 0.0 collective-permute-start.5
  19.4 2.3 %collective-permute-start.4 = (f32[2,40,128]{2,1,0:T(8,128)S(1)}, f32[2,40,128]{2,1,0:T(8,128)S(1)}, u32[]{:S(2)}, u32[]{:S(2)}) collective-permute-start(f32[2,40,128]{2,1,0:T(8,128)S(1)} %pad_maximum_fusion.1), channel_id=1, source_target_pairs={{0,4},{2,6},{4,0},{6,2},{8,12},{10,14},{12,8},{14,10},{1,5},{3,7},... | collective-permute-start | bytes 122888 | tf_op jit(solution)/shard_map/ppermute | solution.py:367
  21.7 2.0 %collective-permute-done.4 = f32[2,40,128]{2,1,0:T(8,128)S(1)} collective-permute-done((f32[2,40,128]{2,1,0:T(8,128)S(1)}, f32[2,40,128]{2,1,0:T(8,128)S(1)}, u32[]{:S(2)}, u32[]{:S(2)}) %collective-permute-start.4) | collective-permute-done | bytes 40992 | tf_op jit(solution)/shard_map/ppermute | solution.py:367
  23.7 0.6 %collective-permute-done.5 = f32[2,40,128]{2,1,0:T(8,128)S(1)} collective-permute-done((f32[2,40,128]{2,1,0:T(8,128)S(1)}, f32[2,40,128]{2,1,0:T(8,128)S(1)}, u32[]{:S(2)}, u32[]{:S(2)}) %collective-permute-start.5) | collective-permute-done | bytes 40992 | tf_op jit(solution)/shard_map/ppermute | solution.py:367
  24.3 0.0 collective-permute-done.6
  24.3 0.1 collective-permute-start.7
  24.4 1.5 %collective-permute-start.9 = (f32[2,32,256]{2,1,0:T(8,128)S(1)}, f32[2,32,256]{2,1,0:T(8,128)S(1)}, u32[]{:S(2)}, u32[]{:S(2)}) collective-permute-start(f32[2,32,256]{2,1,0:T(8,128)S(1)} %get-tuple-element.19), channel_id=1, source_target_pairs={{0,4},{2,14},{4,8},{6,2},{8,12},{10,6},{12,0},{14,10},{1,5},{3,15}... | collective-permute-start | bytes 196616 | tf_op jit(solution)/shard_map/ppermute | solution.py:367
  25.9 4.8 %collective-permute-done.9.far_ref = f32[2,32,256]{2,1,0:T(8,128)S(1)} collective-permute-done((f32[2,32,256]{2,1,0:T(8,128)S(1)}, f32[2,32,256]{2,1,0:T(8,128)S(1)}, u32[]{:S(2)}, u32[]{:S(2)}) %collective-permute-start.9) | collective-permute-done | bytes 65568 | tf_op jit(solution)/shard_map/ppermute | solution.py:367
  30.7 0.0 collective-permute-done.8.cross_ref
  30.7 0.2 shard_map.45
  30.9 0.1 collective-permute-start.10
  31.0 1.3 %collective-permute-done.10.edge_ref = f32[10,8,256]{2,1,0:T(8,128)S(1)} collective-permute-done((f32[10,8,256]{2,1,0:T(8,128)S(1)}, f32[10,8,256]{2,1,0:T(8,128)S(1)}, u32[]{:S(2)}, u32[]{:S(2)}) %collective-permute-start.10) | collective-permute-done | bytes 81952 | tf_op jit(solution)/shard_map/ppermute | solution.py:362
  32.3 1.4 %shard_map.46.detail_ref = f32[4,4,32,256]{3,2,1,0:T(8,128)S(1)} custom-call(f32[4,8,128]{2,1,0:T(8,128)S(1)} %broadcast_in_dim.10.limits_ref, f32[10,32,256]{2,1,0:T(8,128)S(1)} %get-tuple-element.20.coefs_ref, f32[10,8,256]{2,1,0:T(8,128)S(1)} %collective-permute-done.10.edge_ref, f32[32,40]{1,0:T(8,128)S(1)} %get-tuple-element.22.back_y_ref, ...), custom_call_target="tpu_custom_call" | custom-call | flops 20000000 | tf_op jit(solution)/shard_map/pallas_call | solution.py:389
  33.6 0.0 collective-permute-done.7
  33.7 2.6 %shard_map.47 = (f32[4,4,32,256]{3,2,1,0:T(8,128)}, f32[4]{0:T(128)}) custom-call(s32[1]{0:T(128)} %bitcast.place_ref, f32[4,8,128]{2,1,0:T(8,128)S(1)} %broadcast_in_dim.10.limits_ref, f32[2,8,40,128]{3,2,1,0:T(8,128)S(1)} %pad_maximum_fusion.parcels_ref, f32[4,4,32,256]{3,2,1,0:T(8,128)S(1)} %shard_map.46.detail_ref, ...), custom_call_target="tpu_custom_call" | custom-call | flops 100000 | tf_op jit(solution)/shard_map/pallas_call | solution.py:389
  (7 shorter events, 0.0 us)
Async XLA Ops:
  0.6 1.8 %collective-permute-start = (f32[4,32,256]{2,1,0:T(8,128)}, f32[4,32,256]{2,1,0:T(8,128)S(1)}, u32[]{:S(2)}, u32[]{:S(2)}) collective-permute-start(f32[4,32,256]{2,1,0:T(8,128)} %cube_ref.1), channel_id=1, source_target_pairs={{0,1},{1,0},{2,3},{3,2},{4,5},{5,4},{6,7},{7,6},{8,9},{9,8},{10,11... | collective-permute-start | bytes 393224 | tf_op jit(solution)/shard_map/ppermute | solution.py:362
  1.2 0.9 %copy-start = (f32[4,32,256]{2,1,0:T(8,128)S(1)}, f32[4,32,256]{2,1,0:T(8,128)}, u32[]{:S(2)}) copy-start(f32[4,32,256]{2,1,0:T(8,128)} %cube_ref.1) | copy-start | bytes 393220
  2.9 10.3 %copy-start.1 = (f32[4]{0:T(128)S(1)}, f32[4]{0:T(128)}, u32[]{:S(2)}) copy-start(f32[4]{0:T(128)} %param.3) | copy-start | bytes 52
  2.9 8.1 %collective-permute-start.2 = (f32[4,32,256]{2,1,0:T(8,128)S(1)}, f32[4,32,256]{2,1,0:T(8,128)S(1)}, u32[]{:S(2)}, u32[]{:S(2)}) collective-permute-start(f32[4,32,256]{2,1,0:T(8,128)S(1)} %get-tuple-element.17.own_ref), channel_id=1, source_target_pairs={{0,12},{2,6},{4,0},{6,10},{8,4},{10,14},{12,8},{14,2},{1,13},{3,7}... | collective-permute-start | bytes 393224 | tf_op jit(solution)/shard_map/ppermute | solution.py:367
  7.9 5.3 %collective-permute-start.1 = (f32[4,32,256]{2,1,0:T(8,128)S(1)}, f32[4,32,256]{2,1,0:T(8,128)S(1)}, u32[]{:S(2)}, u32[]{:S(2)}) collective-permute-start(f32[4,32,256]{2,1,0:T(8,128)S(1)} %get-tuple-element.17.own_ref), channel_id=1, source_target_pairs={{0,2},{2,0},{4,6},{6,4},{8,10},{10,8},{12,14},{14,12},{1,3},{3,1},... | collective-permute-start | bytes 393224 | tf_op jit(solution)/shard_map/ppermute | solution.py:367
  13.5 3.8 %collective-permute-start.3 = (f32[40,128]{1,0:T(8,128)S(1)}, f32[40,128]{1,0:T(8,128)S(1)}, u32[]{:S(2)}, u32[]{:S(2)}) collective-permute-start(f32[40,128]{1,0:T(8,128)S(1)} %shard_map.44), channel_id=1, source_target_pairs={{0,2},{2,0},{4,6},{6,4},{8,10},{10,8},{12,14},{14,12},{1,3},{3,1},... | collective-permute-start | bytes 61448 | tf_op jit(solution)/shard_map/ppermute | solution.py:367
  13.8 16.9 %collective-permute-start.8 = (f32[4,32,256]{2,1,0:T(8,128)S(1)}, f32[4,32,256]{2,1,0:T(8,128)S(1)}, u32[]{:S(2)}, u32[]{:S(2)}) collective-permute-start(f32[4,32,256]{2,1,0:T(8,128)S(1)} %collective-permute-done.2.level_ref), channel_id=1, source_target_pairs={{0,2},{2,0},{4,6},{6,4},{8,10},{10,8},{12,14},{14,12},{1,3},{3,1},... | collective-permute-start | bytes 393224 | tf_op jit(solution)/shard_map/ppermute | solution.py:367
  17.3 7.0 %collective-permute-start.6 = (f32[2,40,128]{2,1,0:T(8,128)S(1)}, f32[2,40,128]{2,1,0:T(8,128)S(1)}, u32[]{:S(2)}, u32[]{:S(2)}) collective-permute-start(f32[2,40,128]{2,1,0:T(8,128)S(1)} %pad_maximum_fusion.1), channel_id=1, source_target_pairs={{0,12},{2,14},{4,8},{6,10},{8,4},{10,6},{12,0},{14,2},{1,13},{3,15... | collective-permute-start | bytes 122888 | tf_op jit(solution)/shard_map/ppermute | solution.py:367
  19.4 4.9 %collective-permute-start.5 = (f32[2,40,128]{2,1,0:T(8,128)S(1)}, f32[2,40,128]{2,1,0:T(8,128)S(1)}, u32[]{:S(2)}, u32[]{:S(2)}) collective-permute-start(f32[2,40,128]{2,1,0:T(8,128)S(1)} %pad_maximum_fusion.1), channel_id=1, source_target_pairs={{0,8},{2,10},{4,12},{6,14},{8,0},{10,2},{12,4},{14,6},{1,9},{3,11}... | collective-permute-start | bytes 122888 | tf_op jit(solution)/shard_map/ppermute | solution.py:367
  19.4 4.3 %collective-permute-start.4 = (f32[2,40,128]{2,1,0:T(8,128)S(1)}, f32[2,40,128]{2,1,0:T(8,128)S(1)}, u32[]{:S(2)}, u32[]{:S(2)}) collective-permute-start(f32[2,40,128]{2,1,0:T(8,128)S(1)} %pad_maximum_fusion.1), channel_id=1, source_target_pairs={{0,4},{2,6},{4,0},{6,2},{8,12},{10,14},{12,8},{14,10},{1,5},{3,7},... | collective-permute-start | bytes 122888 | tf_op jit(solution)/shard_map/ppermute | solution.py:367
  24.3 9.3 %collective-permute-start.7 = (f32[8,40,128]{2,1,0:T(8,128)S(1)}, f32[8,40,128]{2,1,0:T(8,128)S(1)}, u32[]{:S(2)}, u32[]{:S(2)}) collective-permute-start(f32[8,40,128]{2,1,0:T(8,128)S(1)} %constant_dynamic-update-slice_fusion), channel_id=1, source_target_pairs={{0,1},{1,0},{2,3},{3,2},{4,5},{5,4},{6,7},{7,6},{8,9},{9,8},{10,11... | collective-permute-start | bytes 491528 | tf_op jit(solution)/shard_map/ppermute | solution.py:362
  24.4 6.3 %collective-permute-start.9 = (f32[2,32,256]{2,1,0:T(8,128)S(1)}, f32[2,32,256]{2,1,0:T(8,128)S(1)}, u32[]{:S(2)}, u32[]{:S(2)}) collective-permute-start(f32[2,32,256]{2,1,0:T(8,128)S(1)} %get-tuple-element.19), channel_id=1, source_target_pairs={{0,4},{2,14},{4,8},{6,2},{8,12},{10,6},{12,0},{14,10},{1,5},{3,15}... | collective-permute-start | bytes 196616 | tf_op jit(solution)/shard_map/ppermute | solution.py:367
  30.9 1.3 %collective-permute-start.10 = (f32[10,8,256]{2,1,0:T(8,128)S(1)}, f32[10,8,256]{2,1,0:T(8,128)S(1)}, u32[]{:S(2)}, u32[]{:S(2)}) collective-permute-start(f32[10,8,256]{2,1,0:T(8,128)S(1)} %get-tuple-element.21), channel_id=1, source_target_pairs={{0,1},{1,0},{2,3},{3,2},{4,5},{5,4},{6,7},{7,6},{8,9},{9,8},{10,11... | collective-permute-start | bytes 245768 | tf_op jit(solution)/shard_map/ppermute | solution.py:362

commit v4 on v3

--- a/solution.py
+++ b/solution.py
@@ -137,11 +137,17 @@
         far_ref[z] = jnp.where(odd, head, tail)
 
 
-def tally(value, limit_squares, sums, keep=None):
-    square = value * value
+def tally(values, limit_squares, sums, keep=None):
+    parts = [value * value for value in values]
     for t, limit in enumerate(limit_squares):
-        weight = 1.0 / (square + limit)
-        cut = jnp.minimum(square, limit)
+        bases = [part + limit for part in parts]
+        cuts = [jnp.minimum(part, limit) for part in parts]
+        tops = [1.0] * len(bases)
+        while len(bases) > 1:
+            tops = [tops[i] * bases[i + 1] + tops[i + 1] * bases[i] for i in range(0, len(bases), 2)]
+            bases = [bases[i] * bases[i + 1] for i in range(0, len(bases), 2)]
+        weight = tops[0] / bases[0]
+        cut = functools.reduce(jnp.add, cuts)
         if keep is not None:
             weight = jnp.where(keep, weight, 0.0)
             cut = jnp.where(keep, cut, 0.0)
@@ -170,13 +176,15 @@
             tile = [jnp.where(odd, level[i], own[i]) for i in range(planes)]
             tile += [mate_ref[(i,) + at] for i in range(planes)]
             tile += [jnp.where(odd, own[i], level[i]) for i in range(2)]
+            counted = []
             for k in range(planes // 2):
                 for band in range(2):
                     value = weighted((FILTERS[band][tap], tile[2 * k + tap]) for tap in range(8))
                     if band == 0 and c == 0 and r < lo_rows:
                         lows[pl.ds(k * lo_rows + r, 8), :] = value
                     else:
-                        tally(value, squares, sums)
+                        counted.append(value)
+            tally(counted, squares, sums)
     parcel_ref[pl.ds(0, planes // 2 * lo_rows), :] = dot(lows[...], deep_across_ref[...])
     parcel_ref[pl.ds(planes // 2 * lo_rows, 2 * count), :] = fold(sums)
 
@@ -258,7 +266,7 @@
 
 def final_kernel(
     full, cells, place_ref, limits_ref, parcels_ref, detail_ref, both_y_ref, both_x_ref,
-    out_ref, score_ref, zed, mix, coarse, staged, semaphores,
+    out_ref, score_ref, zed, mix, coarse, staged, scores, semaphores,
 ):
     count, planes, rows, cols = detail_ref.shape
     half_cols = cols // 2
@@ -331,13 +339,18 @@
     for a, kap in enumerate(kappas):
         if not full and kap != 0:
             continue
+        counted = []
         for band in range(2):
             for i in range(0, deep_rows, 8):
                 if not full and i % lo_rows >= lo_rows // 2:
                     continue
-                kept = band == 0 and i < lo_rows
                 value = mix[pl.ds((2 * a + band) * deep_rows + i, 8), :]
-                tally(value, squares, sums, ~low_lanes if kept else None)
+                if band == 0 and i < lo_rows:
+                    tally([value], squares, sums, ~low_lanes)
+                else:
+                    counted.append(value)
+        for i in range(0, len(counted), 2):
+            tally(counted[i : i + 2], squares, sums)
     total = fold(sums)
     if full:
         for side in range(2):
@@ -349,10 +362,12 @@
         weight = jnp.sum(total[t : t + 1] * squares[t][:1])
         residual = jnp.sum(total[count + t : count + t + 1])
         if full:
-            score_ref[t] = cells * residual / (weight * weight)
+            scores[t] = cells * residual / (weight * weight)
         else:
-            score_ref[t] = weight
-            score_ref[count + t] = residual
+            scores[t] = weight
+            scores[count + t] = residual
+    copies.append(pltpu.make_async_copy(scores, score_ref, semaphores.at[count]))
+    copies[-1].start()
     for copy in copies:
         copy.wait()
 
@@ -383,7 +398,7 @@
 def call(kernel, out_shape, smem, vmem, scratches=(), score=False, flops=100_000):
     out_specs = jax.tree.map(lambda _: VMEM, out_shape)
     if score:
-        out_specs = (pl.BlockSpec(memory_space=pltpu.HBM), SMEM)
+        out_specs = (pl.BlockSpec(memory_space=pltpu.HBM),) * 2
 
     def run(*operands):
         return pl.pallas_call(
@@ -474,7 +489,8 @@
             scratch(2 * kappas * rows, half_cols),
             scratch(count * block, half_cols),
             scratch(count, planes, rows, cols),
-            pltpu.SemaphoreType.DMA((count,)),
+            pltpu.SMEM((count if full else 2 * count,), jnp.float32),
+            pltpu.SemaphoreType.DMA((count + 1,)),
         ],
         score=True,
     )(where, limits, parcels, detail, both_y, both_x)

time: 36.4 us -> 35.9 us (0.986)
  Pallas kernels: 5.75 us -> 5.31 us
    pallas_call x7, Pallas kernels: 5.75 us -> 5.31 us  [run(): pl.pallas_call(kernel, out_shape=out_shape, in_specs=[SMEM] * smem + vmem...]
where the time goes in v4:
time: 35.9 us; the launch traced here: 35.8 us
  waiting for transfers between devices  15.1 us (42%)
  starting transfers between devices  13.6 us (38%)
  Pallas kernels  5.31 us (15%)
  local copies, waits for them, and re-layouts  1 us (3%)
  between operations  0.74 us (2%)
    ppermute x8, waiting for transfers between devices, exchanged(): lax.ppermute(array, 'gz', [(i, partner(i) % devices) for i in range(devic...  13.8 us
    ppermute x8, starting transfers between devices, exchanged(): lax.ppermute(array, 'gz', [(i, partner(i) % devices) for i in range(devic...  12.9 us
    pallas_call x7, Pallas kernels, run(): pl.pallas_call(kernel, out_shape=out_shape, in_specs=[SMEM] * smem + vmem...  5.31 us
    ppermute x3, waiting for transfers between devices, shifted(): lax.ppermute(array, axis, [(i, (i + by) % devices) for i in range(devices)])  1.27 us
    unnamed x8, local copies, waits for them, and re-layouts  0.92 us
  transfers between devices with their start and end apart: 11, of which 7 were waited for; matrix products, arithmetic and copies ran while one was open for 0% of the time, Pallas kernels for 7%

profile of v4, /device:TPU:0, one launch (start us, length us, event | category | flops | bytes accessed | tf_op | source)
XLA Modules:
  0.0 35.8 jit_solution(6409455336288975779)
XLA Ops:
  0.6 0.6 %collective-permute-start = (f32[4,32,256]{2,1,0:T(8,128)}, f32[4,32,256]{2,1,0:T(8,128)S(1)}, u32[]{:S(2)}, u32[]{:S(2)}) collective-permute-start(f32[4,32,256]{2,1,0:T(8,128)} %cube_ref.1), channel_id=1, source_target_pairs={{0,1},{1,0},{2,3},{3,2},{4,5},{5,4},{6,7},{7,6},{8,9},{9,8},{10,11... | collective-permute-start | bytes 393224 | tf_op jit(solution)/shard_map/ppermute | solution.py:377
  1.2 0.0 copy-start
  1.2 0.9 %copy-done = f32[4,32,256]{2,1,0:T(8,128)S(1)} copy-done((f32[4,32,256]{2,1,0:T(8,128)S(1)}, f32[4,32,256]{2,1,0:T(8,128)}, u32[]{:S(2)}) %copy-start) | copy-done | bytes 131096
  2.1 0.3 shard_map.41
  2.4 0.0 collective-permute-done.other_ref
  2.4 0.5 %shard_map.42 = (f32[4,32,256]{2,1,0:T(8,128)S(1)}, f32[2,32,256]{2,1,0:T(8,128)S(1)}) custom-call(s32[1]{0:T(128)} %bitcast.place_ref, f32[4,32,256]{2,1,0:T(8,128)S(1)} %get-tuple-element.14.own_ref, f32[4,32,256]{2,1,0:T(8,128)S(1)} %collective-permute-done.other_ref, f32[32,64]{1,0:T(8,128)S(1)} %get-tuple-element.15.y_ref, ...), custom_call_target="tpu_custom_call" | custom-call | flops 100000 | tf_op jit(solution)/shard_map/pallas_call | solution.py:404
  2.9 0.0 copy-start.1
  2.9 5.0 %collective-permute-start.2 = (f32[4,32,256]{2,1,0:T(8,128)S(1)}, f32[4,32,256]{2,1,0:T(8,128)S(1)}, u32[]{:S(2)}, u32[]{:S(2)}) collective-permute-start(f32[4,32,256]{2,1,0:T(8,128)S(1)} %get-tuple-element.17.own_ref), channel_id=1, source_target_pairs={{0,12},{2,6},{4,0},{6,10},{8,4},{10,14},{12,8},{14,2},{1,13},{3,7}... | collective-permute-start | bytes 393224 | tf_op jit(solution)/shard_map/ppermute | solution.py:382
  7.9 0.0 collective-permute-start.1
  7.9 0.6 %shard_map.43 = (f32[256,256]{1,0:T(8,128)S(1)}, f32[128,128]{1,0:T(8,128)S(1)}, bf16[2,128,256]{2,1,0:T(8,128)(2,1)S(1)}, f32[32,40]{1,0:T(8,128)S(1)}, bf16[2,128,128]{2,1,0:T(8,128)(2,1)S(1)}) custom-call(), custom_call_target="tpu_custom_call" | custom-call | flops 100000 | tf_op jit(solution)/shard_map/pallas_call | solution.py:404
  8.5 2.5 %collective-permute-done.2.level_ref = f32[4,32,256]{2,1,0:T(8,128)S(1)} collective-permute-done((f32[4,32,256]{2,1,0:T(8,128)S(1)}, f32[4,32,256]{2,1,0:T(8,128)S(1)}, u32[]{:S(2)}, u32[]{:S(2)}) %collective-permute-start.2) | collective-permute-done | bytes 131104 | tf_op jit(solution)/shard_map/ppermute | solution.py:382
  11.0 2.2 %collective-permute-done.1.mate_ref = f32[4,32,256]{2,1,0:T(8,128)S(1)} collective-permute-done((f32[4,32,256]{2,1,0:T(8,128)S(1)}, f32[4,32,256]{2,1,0:T(8,128)S(1)}, u32[]{:S(2)}, u32[]{:S(2)}) %collective-permute-start.1) | collective-permute-done | bytes 131104 | tf_op jit(solution)/shard_map/ppermute | solution.py:382
  13.2 0.0 copy-done.1
  13.2 0.1 broadcast_in_dim.10.limits_ref
  13.3 0.2 shard_map.44
  13.5 0.3 collective-permute-start.3
  13.8 1.7 %collective-permute-start.8 = (f32[4,32,256]{2,1,0:T(8,128)S(1)}, f32[4,32,256]{2,1,0:T(8,128)S(1)}, u32[]{:S(2)}, u32[]{:S(2)}) collective-permute-start(f32[4,32,256]{2,1,0:T(8,128)S(1)} %collective-permute-done.2.level_ref), channel_id=1, source_target_pairs={{0,2},{2,0},{4,6},{6,4},{8,10},{10,8},{12,14},{14,12},{1,3},{3,1},... | collective-permute-start | bytes 393224 | tf_op jit(solution)/shard_map/ppermute | solution.py:382
  15.6 1.8 %collective-permute-done.3 = f32[40,128]{1,0:T(8,128)S(1)} collective-permute-done((f32[40,128]{1,0:T(8,128)S(1)}, f32[40,128]{1,0:T(8,128)S(1)}, u32[]{:S(2)}, u32[]{:S(2)}) %collective-permute-start.3) | collective-permute-done | bytes 20512 | tf_op jit(solution)/shard_map/ppermute | solution.py:382
  17.3 2.1 %collective-permute-start.6 = (f32[2,40,128]{2,1,0:T(8,128)S(1)}, f32[2,40,128]{2,1,0:T(8,128)S(1)}, u32[]{:S(2)}, u32[]{:S(2)}) collective-permute-start(f32[2,40,128]{2,1,0:T(8,128)S(1)} %pad_maximum_fusion.1), channel_id=1, source_target_pairs={{0,12},{2,14},{4,8},{6,10},{8,4},{10,6},{12,0},{14,2},{1,13},{3,15... | collective-permute-start | bytes 122888 | tf_op jit(solution)/shard_map/ppermute | solution.py:382
  19.4 0.0 collective-permute-start.5
  19.4 2.3 %collective-permute-start.4 = (f32[2,40,128]{2,1,0:T(8,128)S(1)}, f32[2,40,128]{2,1,0:T(8,128)S(1)}, u32[]{:S(2)}, u32[]{:S(2)}) collective-permute-start(f32[2,40,128]{2,1,0:T(8,128)S(1)} %pad_maximum_fusion.1), channel_id=1, source_target_pairs={{0,4},{2,6},{4,0},{6,2},{8,12},{10,14},{12,8},{14,10},{1,5},{3,7},... | collective-permute-start | bytes 122888 | tf_op jit(solution)/shard_map/ppermute | solution.py:382
  21.7 2.0 %collective-permute-done.4 = f32[2,40,128]{2,1,0:T(8,128)S(1)} collective-permute-done((f32[2,40,128]{2,1,0:T(8,128)S(1)}, f32[2,40,128]{2,1,0:T(8,128)S(1)}, u32[]{:S(2)}, u32[]{:S(2)}) %collective-permute-start.4) | collective-permute-done | bytes 40992 | tf_op jit(solution)/shard_map/ppermute | solution.py:382
  23.7 0.6 %collective-permute-done.5 = f32[2,40,128]{2,1,0:T(8,128)S(1)} collective-permute-done((f32[2,40,128]{2,1,0:T(8,128)S(1)}, f32[2,40,128]{2,1,0:T(8,128)S(1)}, u32[]{:S(2)}, u32[]{:S(2)}) %collective-permute-start.5) | collective-permute-done | bytes 40992 | tf_op jit(solution)/shard_map/ppermute | solution.py:382
  24.3 0.0 collective-permute-done.6
  24.4 0.1 collective-permute-start.7
  24.4 1.5 %collective-permute-start.9 = (f32[2,32,256]{2,1,0:T(8,128)S(1)}, f32[2,32,256]{2,1,0:T(8,128)S(1)}, u32[]{:S(2)}, u32[]{:S(2)}) collective-permute-start(f32[2,32,256]{2,1,0:T(8,128)S(1)} %get-tuple-element.19), channel_id=1, source_target_pairs={{0,4},{2,14},{4,8},{6,2},{8,12},{10,6},{12,0},{14,10},{1,5},{3,15}... | collective-permute-start | bytes 196616 | tf_op jit(solution)/shard_map/ppermute | solution.py:382
  25.9 4.8 %collective-permute-done.9.far_ref = f32[2,32,256]{2,1,0:T(8,128)S(1)} collective-permute-done((f32[2,32,256]{2,1,0:T(8,128)S(1)}, f32[2,32,256]{2,1,0:T(8,128)S(1)}, u32[]{:S(2)}, u32[]{:S(2)}) %collective-permute-start.9) | collective-permute-done | bytes 65568 | tf_op jit(solution)/shard_map/ppermute | solution.py:382
  30.7 0.0 collective-permute-done.8.cross_ref
  30.7 0.2 shard_map.45
  30.9 0.1 collective-permute-start.10
  31.0 1.3 %collective-permute-done.10.edge_ref = f32[10,8,256]{2,1,0:T(8,128)S(1)} collective-permute-done((f32[10,8,256]{2,1,0:T(8,128)S(1)}, f32[10,8,256]{2,1,0:T(8,128)S(1)}, u32[]{:S(2)}, u32[]{:S(2)}) %collective-permute-start.10) | collective-permute-done | bytes 81952 | tf_op jit(solution)/shard_map/ppermute | solution.py:377
  32.3 1.4 %shard_map.46.detail_ref = f32[4,4,32,256]{3,2,1,0:T(8,128)S(1)} custom-call(f32[4,8,128]{2,1,0:T(8,128)S(1)} %broadcast_in_dim.10.limits_ref, f32[10,32,256]{2,1,0:T(8,128)S(1)} %get-tuple-element.20.coefs_ref, f32[10,8,256]{2,1,0:T(8,128)S(1)} %collective-permute-done.10.edge_ref, f32[32,40]{1,0:T(8,128)S(1)} %get-tuple-element.22.back_y_ref, ...), custom_call_target="tpu_custom_call" | custom-call | flops 20000000 | tf_op jit(solution)/shard_map/pallas_call | solution.py:404
  33.6 0.0 collective-permute-done.7
  33.7 2.1 %shard_map.47 = (f32[4,4,32,256]{3,2,1,0:T(8,128)}, f32[4]{0:T(128)}) custom-call(s32[1]{0:T(128)} %bitcast.place_ref, f32[4,8,128]{2,1,0:T(8,128)S(1)} %broadcast_in_dim.10.limits_ref, f32[2,8,40,128]{3,2,1,0:T(8,128)S(1)} %pad_maximum_fusion.parcels_ref, f32[4,4,32,256]{3,2,1,0:T(8,128)S(1)} %shard_map.46.detail_ref, ...), custom_call_target="tpu_custom_call" | custom-call | flops 100000 | tf_op jit(solution)/shard_map/pallas_call | solution.py:404
  (7 shorter events, 0.0 us)
Async XLA Ops:
  0.6 1.8 %collective-permute-start = (f32[4,32,256]{2,1,0:T(8,128)}, f32[4,32,256]{2,1,0:T(8,128)S(1)}, u32[]{:S(2)}, u32[]{:S(2)}) collective-permute-start(f32[4,32,256]{2,1,0:T(8,128)} %cube_ref.1), channel_id=1, source_target_pairs={{0,1},{1,0},{2,3},{3,2},{4,5},{5,4},{6,7},{7,6},{8,9},{9,8},{10,11... | collective-permute-start | bytes 393224 | tf_op jit(solution)/shard_map/ppermute | solution.py:377
  1.2 0.9 %copy-start = (f32[4,32,256]{2,1,0:T(8,128)S(1)}, f32[4,32,256]{2,1,0:T(8,128)}, u32[]{:S(2)}) copy-start(f32[4,32,256]{2,1,0:T(8,128)} %cube_ref.1) | copy-start | bytes 393220
  2.9 10.3 %copy-start.1 = (f32[4]{0:T(128)S(1)}, f32[4]{0:T(128)}, u32[]{:S(2)}) copy-start(f32[4]{0:T(128)} %param.3) | copy-start | bytes 52
  2.9 8.1 %collective-permute-start.2 = (f32[4,32,256]{2,1,0:T(8,128)S(1)}, f32[4,32,256]{2,1,0:T(8,128)S(1)}, u32[]{:S(2)}, u32[]{:S(2)}) collective-permute-start(f32[4,32,256]{2,1,0:T(8,128)S(1)} %get-tuple-element.17.own_ref), channel_id=1, source_target_pairs={{0,12},{2,6},{4,0},{6,10},{8,4},{10,14},{12,8},{14,2},{1,13},{3,7}... | collective-permute-start | bytes 393224 | tf_op jit(solution)/shard_map/ppermute | solution.py:382
  7.9 5.3 %collective-permute-start.1 = (f32[4,32,256]{2,1,0:T(8,128)S(1)}, f32[4,32,256]{2,1,0:T(8,128)S(1)}, u32[]{:S(2)}, u32[]{:S(2)}) collective-permute-start(f32[4,32,256]{2,1,0:T(8,128)S(1)} %get-tuple-element.17.own_ref), channel_id=1, source_target_pairs={{0,2},{2,0},{4,6},{6,4},{8,10},{10,8},{12,14},{14,12},{1,3},{3,1},... | collective-permute-start | bytes 393224 | tf_op jit(solution)/shard_map/ppermute | solution.py:382
  13.5 3.8 %collective-permute-start.3 = (f32[40,128]{1,0:T(8,128)S(1)}, f32[40,128]{1,0:T(8,128)S(1)}, u32[]{:S(2)}, u32[]{:S(2)}) collective-permute-start(f32[40,128]{1,0:T(8,128)S(1)} %shard_map.44), channel_id=1, source_target_pairs={{0,2},{2,0},{4,6},{6,4},{8,10},{10,8},{12,14},{14,12},{1,3},{3,1},... | collective-permute-start | bytes 61448 | tf_op jit(solution)/shard_map/ppermute | solution.py:382
  13.8 16.9 %collective-permute-start.8 = (f32[4,32,256]{2,1,0:T(8,128)S(1)}, f32[4,32,256]{2,1,0:T(8,128)S(1)}, u32[]{:S(2)}, u32[]{:S(2)}) collective-permute-start(f32[4,32,256]{2,1,0:T(8,128)S(1)} %collective-permute-done.2.level_ref), channel_id=1, source_target_pairs={{0,2},{2,0},{4,6},{6,4},{8,10},{10,8},{12,14},{14,12},{1,3},{3,1},... | collective-permute-start | bytes 393224 | tf_op jit(solution)/shard_map/ppermute | solution.py:382
  17.3 7.0 %collective-permute-start.6 = (f32[2,40,128]{2,1,0:T(8,128)S(1)}, f32[2,40,128]{2,1,0:T(8,128)S(1)}, u32[]{:S(2)}, u32[]{:S(2)}) collective-permute-start(f32[2,40,128]{2,1,0:T(8,128)S(1)} %pad_maximum_fusion.1), channel_id=1, source_target_pairs={{0,12},{2,14},{4,8},{6,10},{8,4},{10,6},{12,0},{14,2},{1,13},{3,15... | collective-permute-start | bytes 122888 | tf_op jit(solution)/shard_map/ppermute | solution.py:382
  19.4 4.9 %collective-permute-start.5 = (f32[2,40,128]{2,1,0:T(8,128)S(1)}, f32[2,40,128]{2,1,0:T(8,128)S(1)}, u32[]{:S(2)}, u32[]{:S(2)}) collective-permute-start(f32[2,40,128]{2,1,0:T(8,128)S(1)} %pad_maximum_fusion.1), channel_id=1, source_target_pairs={{0,8},{2,10},{4,12},{6,14},{8,0},{10,2},{12,4},{14,6},{1,9},{3,11}... | collective-permute-start | bytes 122888 | tf_op jit(solution)/shard_map/ppermute | solution.py:382
  19.4 4.3 %collective-permute-start.4 = (f32[2,40,128]{2,1,0:T(8,128)S(1)}, f32[2,40,128]{2,1,0:T(8,128)S(1)}, u32[]{:S(2)}, u32[]{:S(2)}) collective-permute-start(f32[2,40,128]{2,1,0:T(8,128)S(1)} %pad_maximum_fusion.1), channel_id=1, source_target_pairs={{0,4},{2,6},{4,0},{6,2},{8,12},{10,14},{12,8},{14,10},{1,5},{3,7},... | collective-permute-start | bytes 122888 | tf_op jit(solution)/shard_map/ppermute | solution.py:382
  24.4 9.3 %collective-permute-start.7 = (f32[8,40,128]{2,1,0:T(8,128)S(1)}, f32[8,40,128]{2,1,0:T(8,128)S(1)}, u32[]{:S(2)}, u32[]{:S(2)}) collective-permute-start(f32[8,40,128]{2,1,0:T(8,128)S(1)} %constant_dynamic-update-slice_fusion), channel_id=1, source_target_pairs={{0,1},{1,0},{2,3},{3,2},{4,5},{5,4},{6,7},{7,6},{8,9},{9,8},{10,11... | collective-permute-start | bytes 491528 | tf_op jit(solution)/shard_map/ppermute | solution.py:377
  24.4 6.3 %collective-permute-start.9 = (f32[2,32,256]{2,1,0:T(8,128)S(1)}, f32[2,32,256]{2,1,0:T(8,128)S(1)}, u32[]{:S(2)}, u32[]{:S(2)}) collective-permute-start(f32[2,32,256]{2,1,0:T(8,128)S(1)} %get-tuple-element.19), channel_id=1, source_target_pairs={{0,4},{2,14},{4,8},{6,2},{8,12},{10,6},{12,0},{14,10},{1,5},{3,15}... | collective-permute-start | bytes 196616 | tf_op jit(solution)/shard_map/ppermute | solution.py:382
  30.9 1.3 %collective-permute-start.10 = (f32[10,8,256]{2,1,0:T(8,128)S(1)}, f32[10,8,256]{2,1,0:T(8,128)S(1)}, u32[]{:S(2)}, u32[]{:S(2)}) collective-permute-start(f32[10,8,256]{2,1,0:T(8,128)S(1)} %get-tuple-element.21), channel_id=1, source_target_pairs={{0,1},{1,0},{2,3},{3,2},{4,5},{5,4},{6,7},{7,6},{8,9},{9,8},{10,11... | collective-permute-start | bytes 245768 | tf_op jit(solution)/shard_map/ppermute | solution.py:377

commit v5 on v4

--- a/solution.py
+++ b/solution.py
@@ -280,9 +280,9 @@
     here = place_ref[0]
 
     def piece(spot):
-        spot = here + pieces + spot
+        spot = here + 2 * pieces + spot
         if not full:
-            return spot + 2 * (spot % 2) - here - pieces + 5
+            return spot + 2 * (spot % 2) - here - 2 * pieces + 5
         owner = (spot + 2 * (spot % 2)) % pieces
         return ((owner // 2) ^ (here // 2)) * 2 + ((owner % 2) ^ (here % 2))
 
@@ -313,6 +313,40 @@
     both_x = (both_x_ref[0], both_x_ref[1])
     copies = []
     for t in range(count):
+        if t == count - 1:
+            sums = [[None] * count, [None] * count]
+            for a, kap in enumerate(kappas):
+                if not full and kap != 0:
+                    continue
+                counted = []
+                for band in range(2):
+                    for i in range(0, deep_rows, 8):
+                        if not full and i % lo_rows >= lo_rows // 2:
+                            continue
+                        value = mix[pl.ds((2 * a + band) * deep_rows + i, 8), :]
+                        if band == 0 and i < lo_rows:
+                            tally([value], squares, sums, ~low_lanes)
+                        else:
+                            counted.append(value)
+                for i in range(0, len(counted), 2):
+                    tally(counted[i : i + 2], squares, sums)
+            total = fold(sums)
+            if full:
+                for side in range(2):
+                    for at in range(pieces):
+                        total = total + parcels_ref[side, at, pl.ds(depth * lo_rows, 2 * count), :]
+            else:
+                total = total + parcels_ref[0, 5, pl.ds(depth * lo_rows, 2 * count), :]
+            for u in range(count):
+                weight = jnp.sum(total[u : u + 1] * squares[u][:1])
+                residual = jnp.sum(total[count + u : count + u + 1])
+                if full:
+                    scores[u] = cells * residual / (weight * weight)
+                else:
+                    scores[u] = weight
+                    scores[count + u] = residual
+            copies.append(pltpu.make_async_copy(scores, score_ref, semaphores.at[count]))
+            copies[-1].start()
         for i in range(0, deep_rows, 8):
             shrunk = {}
             for a, kap in enumerate(kappas):
@@ -335,39 +369,6 @@
         copies.append(pltpu.make_async_copy(staged.at[t], out_ref.at[:, t], semaphores.at[t]))
         copies[-1].start()
 
-    sums = [[None] * count, [None] * count]
-    for a, kap in enumerate(kappas):
-        if not full and kap != 0:
-            continue
-        counted = []
-        for band in range(2):
-            for i in range(0, deep_rows, 8):
-                if not full and i % lo_rows >= lo_rows // 2:
-                    continue
-                value = mix[pl.ds((2 * a + band) * deep_rows + i, 8), :]
-                if band == 0 and i < lo_rows:
-                    tally([value], squares, sums, ~low_lanes)
-                else:
-                    counted.append(value)
-        for i in range(0, len(counted), 2):
-            tally(counted[i : i + 2], squares, sums)
-    total = fold(sums)
-    if full:
-        for side in range(2):
-            for at in range(pieces):
-                total = total + parcels_ref[side, at, pl.ds(depth * lo_rows, 2 * count), :]
-    else:
-        total = total + parcels_ref[0, 5, pl.ds(depth * lo_rows, 2 * count), :]
-    for t in range(count):
-        weight = jnp.sum(total[t : t + 1] * squares[t][:1])
-        residual = jnp.sum(total[count + t : count + t + 1])
-        if full:
-            scores[t] = cells * residual / (weight * weight)
-        else:
-            scores[t] = weight
-            scores[count + t] = residual
-    copies.append(pltpu.make_async_copy(scores, score_ref, semaphores.at[count]))
-    copies[-1].start()
     for copy in copies:
         copy.wait()
 
@@ -434,7 +435,7 @@
         (
             struct(cols, cols), struct(rows, 2 * rows), struct(planes, rows, cols),
         ), 0, [pl.BlockSpec(memory_space=pltpu.HBM)], [pltpu.SemaphoreType.DMA],
-    )(noisy_cube)
+    )(pltpu.with_memory_space_constraint(noisy_cube, pltpu.HBM))
     flat, far = call(
         plane_kernel, (struct(planes, rows, cols), struct(2, rows, cols)), 1, [VMEM] * 4,
         [scratch(planes * rows, cols)],

time: 35.9 us -> 35.9 us (level)
  local copies, waits for them, and re-layouts: 1 us -> 0.1 us
  Pallas kernels: 5.31 us -> 5.92 us
    unnamed x8 -> x6, local copies, waits for them, and re-layouts: 0.92 us -> 0.02 us
    pallas_call x7, Pallas kernels: 5.31 us -> 5.92 us  [run(): pl.pallas_call(kernel, out_shape=out_shape, in_specs=[SMEM] * smem + vmem...]
  transfers between devices with their start and end apart: 11 -> 11, of which waited for: 7 -> 8; matrix products, arithmetic and copies ran while one was open for 0% -> 0% of each run, Pallas kernels for 7% -> 9%
where the time goes in v5:
time: 35.9 us; the launch traced here: 35.8 us
  waiting for transfers between devices  15.3 us (43%)
  starting transfers between devices  13.7 us (38%)
  Pallas kernels  5.92 us (16%)
  between operations  0.73 us (2%)
    ppermute x8, waiting for transfers between devices, exchanged(): lax.ppermute(array, 'gz', [(i, partner(i) % devices) for i in range(devic...  13.8 us
    ppermute x8, starting transfers between devices, exchanged(): lax.ppermute(array, 'gz', [(i, partner(i) % devices) for i in range(devic...  13 us
    pallas_call x7, Pallas kernels, run(): pl.pallas_call(kernel, out_shape=out_shape, in_specs=[SMEM] * smem + vmem...  5.92 us
    ppermute x3, waiting for transfers between devices, shifted(): lax.ppermute(array, axis, [(i, (i + by) % devices) for i in range(devices)])  1.54 us
  transfers between devices with their start and end apart: 11, of which 8 were waited for; matrix products, arithmetic and copies ran while one was open for 0% of the time, Pallas kernels for 9%

profile of v5, /device:TPU:0, one launch (start us, length us, event | category | flops | bytes accessed | tf_op | source)
XLA Modules:
  0.0 35.8 jit_solution(6230021281705304511)
XLA Ops:
  0.6 0.6 %collective-permute-start = (f32[4,32,256]{2,1,0:T(8,128)}, f32[4,32,256]{2,1,0:T(8,128)S(1)}, u32[]{:S(2)}, u32[]{:S(2)}) collective-permute-start(f32[4,32,256]{2,1,0:T(8,128)} %cube_ref.1), channel_id=1, source_target_pairs={{0,1},{1,0},{2,3},{3,2},{4,5},{5,4},{6,7},{7,6},{8,9},{9,8},{10,11... | collective-permute-start | bytes 393224 | tf_op jit(solution)/shard_map/ppermute | solution.py:378
  1.2 0.9 %shard_map.41 = (f32[256,256]{1,0:T(8,128)S(1)}, f32[32,64]{1,0:T(8,128)S(1)}, f32[4,32,256]{2,1,0:T(8,128)S(1)}) custom-call(f32[4,32,256]{2,1,0:T(8,128)} %cube_ref.1), custom_call_target="tpu_custom_call" | custom-call | flops 100000 | tf_op jit(solution)/shard_map/pallas_call | solution.py:405
  2.1 0.3 collective-permute-done.other_ref
  2.4 0.5 %shard_map.42 = (f32[4,32,256]{2,1,0:T(8,128)S(1)}, f32[2,32,256]{2,1,0:T(8,128)S(1)}) custom-call(s32[1]{0:T(128)} %bitcast.place_ref, f32[4,32,256]{2,1,0:T(8,128)S(1)} %get-tuple-element.14.own_ref, f32[4,32,256]{2,1,0:T(8,128)S(1)} %collective-permute-done.other_ref, f32[32,64]{1,0:T(8,128)S(1)} %get-tuple-element.15.y_ref, ...), custom_call_target="tpu_custom_call" | custom-call | flops 100000 | tf_op jit(solution)/shard_map/pallas_call | solution.py:405
  2.9 0.0 copy-start
  2.9 5.0 %collective-permute-start.2 = (f32[4,32,256]{2,1,0:T(8,128)S(1)}, f32[4,32,256]{2,1,0:T(8,128)S(1)}, u32[]{:S(2)}, u32[]{:S(2)}) collective-permute-start(f32[4,32,256]{2,1,0:T(8,128)S(1)} %get-tuple-element.17.own_ref), channel_id=1, source_target_pairs={{0,12},{2,6},{4,0},{6,10},{8,4},{10,14},{12,8},{14,2},{1,13},{3,7}... | collective-permute-start | bytes 393224 | tf_op jit(solution)/shard_map/ppermute | solution.py:383
  7.9 0.0 collective-permute-start.1
  7.9 0.6 %shard_map.43 = (f32[256,256]{1,0:T(8,128)S(1)}, f32[128,128]{1,0:T(8,128)S(1)}, bf16[2,128,256]{2,1,0:T(8,128)(2,1)S(1)}, f32[32,40]{1,0:T(8,128)S(1)}, bf16[2,128,128]{2,1,0:T(8,128)(2,1)S(1)}) custom-call(), custom_call_target="tpu_custom_call" | custom-call | flops 100000 | tf_op jit(solution)/shard_map/pallas_call | solution.py:405
  8.5 2.4 %collective-permute-done.2.level_ref = f32[4,32,256]{2,1,0:T(8,128)S(1)} collective-permute-done((f32[4,32,256]{2,1,0:T(8,128)S(1)}, f32[4,32,256]{2,1,0:T(8,128)S(1)}, u32[]{:S(2)}, u32[]{:S(2)}) %collective-permute-start.2) | collective-permute-done | bytes 131104 | tf_op jit(solution)/shard_map/ppermute | solution.py:383
  10.9 2.2 %collective-permute-done.1.mate_ref = f32[4,32,256]{2,1,0:T(8,128)S(1)} collective-permute-done((f32[4,32,256]{2,1,0:T(8,128)S(1)}, f32[4,32,256]{2,1,0:T(8,128)S(1)}, u32[]{:S(2)}, u32[]{:S(2)}) %collective-permute-start.1) | collective-permute-done | bytes 131104 | tf_op jit(solution)/shard_map/ppermute | solution.py:383
  13.1 0.0 copy-done
  13.1 0.1 broadcast_in_dim.10.limits_ref
  13.2 0.2 shard_map.44
  13.4 0.3 collective-permute-start.3
  13.8 1.7 %collective-permute-start.8 = (f32[4,32,256]{2,1,0:T(8,128)S(1)}, f32[4,32,256]{2,1,0:T(8,128)S(1)}, u32[]{:S(2)}, u32[]{:S(2)}) collective-permute-start(f32[4,32,256]{2,1,0:T(8,128)S(1)} %collective-permute-done.2.level_ref), channel_id=1, source_target_pairs={{0,2},{2,0},{4,6},{6,4},{8,10},{10,8},{12,14},{14,12},{1,3},{3,1},... | collective-permute-start | bytes 393224 | tf_op jit(solution)/shard_map/ppermute | solution.py:383
  15.5 1.8 %collective-permute-done.3 = f32[40,128]{1,0:T(8,128)S(1)} collective-permute-done((f32[40,128]{1,0:T(8,128)S(1)}, f32[40,128]{1,0:T(8,128)S(1)}, u32[]{:S(2)}, u32[]{:S(2)}) %collective-permute-start.3) | collective-permute-done | bytes 20512 | tf_op jit(solution)/shard_map/ppermute | solution.py:383
  17.3 2.1 %collective-permute-start.6 = (f32[2,40,128]{2,1,0:T(8,128)S(1)}, f32[2,40,128]{2,1,0:T(8,128)S(1)}, u32[]{:S(2)}, u32[]{:S(2)}) collective-permute-start(f32[2,40,128]{2,1,0:T(8,128)S(1)} %pad_maximum_fusion.1), channel_id=1, source_target_pairs={{0,12},{2,14},{4,8},{6,10},{8,4},{10,6},{12,0},{14,2},{1,13},{3,15... | collective-permute-start | bytes 122888 | tf_op jit(solution)/shard_map/ppermute | solution.py:383
  19.4 0.0 collective-permute-start.5
  19.4 2.3 %collective-permute-start.4 = (f32[2,40,128]{2,1,0:T(8,128)S(1)}, f32[2,40,128]{2,1,0:T(8,128)S(1)}, u32[]{:S(2)}, u32[]{:S(2)}) collective-permute-start(f32[2,40,128]{2,1,0:T(8,128)S(1)} %pad_maximum_fusion.1), channel_id=1, source_target_pairs={{0,4},{2,6},{4,0},{6,2},{8,12},{10,14},{12,8},{14,10},{1,5},{3,7},... | collective-permute-start | bytes 122888 | tf_op jit(solution)/shard_map/ppermute | solution.py:383
  21.7 2.0 %collective-permute-done.4 = f32[2,40,128]{2,1,0:T(8,128)S(1)} collective-permute-done((f32[2,40,128]{2,1,0:T(8,128)S(1)}, f32[2,40,128]{2,1,0:T(8,128)S(1)}, u32[]{:S(2)}, u32[]{:S(2)}) %collective-permute-start.4) | collective-permute-done | bytes 40992 | tf_op jit(solution)/shard_map/ppermute | solution.py:383
  23.7 0.6 %collective-permute-done.5 = f32[2,40,128]{2,1,0:T(8,128)S(1)} collective-permute-done((f32[2,40,128]{2,1,0:T(8,128)S(1)}, f32[2,40,128]{2,1,0:T(8,128)S(1)}, u32[]{:S(2)}, u32[]{:S(2)}) %collective-permute-start.5) | collective-permute-done | bytes 40992 | tf_op jit(solution)/shard_map/ppermute | solution.py:383
  24.3 0.0 collective-permute-done.6
  24.3 0.1 collective-permute-start.7
  24.4 1.5 %collective-permute-start.9 = (f32[2,32,256]{2,1,0:T(8,128)S(1)}, f32[2,32,256]{2,1,0:T(8,128)S(1)}, u32[]{:S(2)}, u32[]{:S(2)}) collective-permute-start(f32[2,32,256]{2,1,0:T(8,128)S(1)} %get-tuple-element.19), channel_id=1, source_target_pairs={{0,4},{2,14},{4,8},{6,2},{8,12},{10,6},{12,0},{14,10},{1,5},{3,15}... | collective-permute-start | bytes 196616 | tf_op jit(solution)/shard_map/ppermute | solution.py:383
  25.9 4.8 %collective-permute-done.9.far_ref = f32[2,32,256]{2,1,0:T(8,128)S(1)} collective-permute-done((f32[2,32,256]{2,1,0:T(8,128)S(1)}, f32[2,32,256]{2,1,0:T(8,128)S(1)}, u32[]{:S(2)}, u32[]{:S(2)}) %collective-permute-start.9) | collective-permute-done | bytes 65568 | tf_op jit(solution)/shard_map/ppermute | solution.py:383
  30.7 0.0 collective-permute-done.8.cross_ref
  30.7 0.2 shard_map.45
  30.9 0.1 collective-permute-start.10
  31.0 1.3 %collective-permute-done.10.edge_ref = f32[10,8,256]{2,1,0:T(8,128)S(1)} collective-permute-done((f32[10,8,256]{2,1,0:T(8,128)S(1)}, f32[10,8,256]{2,1,0:T(8,128)S(1)}, u32[]{:S(2)}, u32[]{:S(2)}) %collective-permute-start.10) | collective-permute-done | bytes 81952 | tf_op jit(solution)/shard_map/ppermute | solution.py:378
  32.2 1.4 %shard_map.46.detail_ref = f32[4,4,32,256]{3,2,1,0:T(8,128)S(1)} custom-call(f32[4,8,128]{2,1,0:T(8,128)S(1)} %broadcast_in_dim.10.limits_ref, f32[10,32,256]{2,1,0:T(8,128)S(1)} %get-tuple-element.20.coefs_ref, f32[10,8,256]{2,1,0:T(8,128)S(1)} %collective-permute-done.10.edge_ref, f32[32,40]{1,0:T(8,128)S(1)} %get-tuple-element.22.back_y_ref, ...), custom_call_target="tpu_custom_call" | custom-call | flops 20000000 | tf_op jit(solution)/shard_map/pallas_call | solution.py:405
  33.6 0.0 collective-permute-done.7
  33.6 2.1 %shard_map.47 = (f32[4,4,32,256]{3,2,1,0:T(8,128)}, f32[4]{0:T(128)}) custom-call(s32[1]{0:T(128)} %bitcast.place_ref, f32[4,8,128]{2,1,0:T(8,128)S(1)} %broadcast_in_dim.10.limits_ref, f32[2,8,40,128]{3,2,1,0:T(8,128)S(1)} %pad_maximum_fusion.parcels_ref, f32[4,4,32,256]{3,2,1,0:T(8,128)S(1)} %shard_map.46.detail_ref, ...), custom_call_target="tpu_custom_call" | custom-call | flops 100000 | tf_op jit(solution)/shard_map/pallas_call | solution.py:405
  (7 shorter events, 0.0 us)
Async XLA Ops:
  0.6 1.8 %collective-permute-start = (f32[4,32,256]{2,1,0:T(8,128)}, f32[4,32,256]{2,1,0:T(8,128)S(1)}, u32[]{:S(2)}, u32[]{:S(2)}) collective-permute-start(f32[4,32,256]{2,1,0:T(8,128)} %cube_ref.1), channel_id=1, source_target_pairs={{0,1},{1,0},{2,3},{3,2},{4,5},{5,4},{6,7},{7,6},{8,9},{9,8},{10,11... | collective-permute-start | bytes 393224 | tf_op jit(solution)/shard_map/ppermute | solution.py:378
  2.9 10.3 %copy-start = (f32[4]{0:T(128)S(1)}, f32[4]{0:T(128)}, u32[]{:S(2)}) copy-start(f32[4]{0:T(128)} %param.3) | copy-start | bytes 52
  2.9 8.1 %collective-permute-start.2 = (f32[4,32,256]{2,1,0:T(8,128)S(1)}, f32[4,32,256]{2,1,0:T(8,128)S(1)}, u32[]{:S(2)}, u32[]{:S(2)}) collective-permute-start(f32[4,32,256]{2,1,0:T(8,128)S(1)} %get-tuple-element.17.own_ref), channel_id=1, source_target_pairs={{0,12},{2,6},{4,0},{6,10},{8,4},{10,14},{12,8},{14,2},{1,13},{3,7}... | collective-permute-start | bytes 393224 | tf_op jit(solution)/shard_map/ppermute | solution.py:383
  7.9 5.3 %collective-permute-start.1 = (f32[4,32,256]{2,1,0:T(8,128)S(1)}, f32[4,32,256]{2,1,0:T(8,128)S(1)}, u32[]{:S(2)}, u32[]{:S(2)}) collective-permute-start(f32[4,32,256]{2,1,0:T(8,128)S(1)} %get-tuple-element.17.own_ref), channel_id=1, source_target_pairs={{0,2},{2,0},{4,6},{6,4},{8,10},{10,8},{12,14},{14,12},{1,3},{3,1},... | collective-permute-start | bytes 393224 | tf_op jit(solution)/shard_map/ppermute | solution.py:383
  13.4 3.8 %collective-permute-start.3 = (f32[40,128]{1,0:T(8,128)S(1)}, f32[40,128]{1,0:T(8,128)S(1)}, u32[]{:S(2)}, u32[]{:S(2)}) collective-permute-start(f32[40,128]{1,0:T(8,128)S(1)} %shard_map.44), channel_id=1, source_target_pairs={{0,2},{2,0},{4,6},{6,4},{8,10},{10,8},{12,14},{14,12},{1,3},{3,1},... | collective-permute-start | bytes 61448 | tf_op jit(solution)/shard_map/ppermute | solution.py:383
  13.8 16.9 %collective-permute-start.8 = (f32[4,32,256]{2,1,0:T(8,128)S(1)}, f32[4,32,256]{2,1,0:T(8,128)S(1)}, u32[]{:S(2)}, u32[]{:S(2)}) collective-permute-start(f32[4,32,256]{2,1,0:T(8,128)S(1)} %collective-permute-done.2.level_ref), channel_id=1, source_target_pairs={{0,2},{2,0},{4,6},{6,4},{8,10},{10,8},{12,14},{14,12},{1,3},{3,1},... | collective-permute-start | bytes 393224 | tf_op jit(solution)/shard_map/ppermute | solution.py:383
  17.3 7.0 %collective-permute-start.6 = (f32[2,40,128]{2,1,0:T(8,128)S(1)}, f32[2,40,128]{2,1,0:T(8,128)S(1)}, u32[]{:S(2)}, u32[]{:S(2)}) collective-permute-start(f32[2,40,128]{2,1,0:T(8,128)S(1)} %pad_maximum_fusion.1), channel_id=1, source_target_pairs={{0,12},{2,14},{4,8},{6,10},{8,4},{10,6},{12,0},{14,2},{1,13},{3,15... | collective-permute-start | bytes 122888 | tf_op jit(solution)/shard_map/ppermute | solution.py:383
  19.4 4.9 %collective-permute-start.5 = (f32[2,40,128]{2,1,0:T(8,128)S(1)}, f32[2,40,128]{2,1,0:T(8,128)S(1)}, u32[]{:S(2)}, u32[]{:S(2)}) collective-permute-start(f32[2,40,128]{2,1,0:T(8,128)S(1)} %pad_maximum_fusion.1), channel_id=1, source_target_pairs={{0,8},{2,10},{4,12},{6,14},{8,0},{10,2},{12,4},{14,6},{1,9},{3,11}... | collective-permute-start | bytes 122888 | tf_op jit(solution)/shard_map/ppermute | solution.py:383
  19.4 4.3 %collective-permute-start.4 = (f32[2,40,128]{2,1,0:T(8,128)S(1)}, f32[2,40,128]{2,1,0:T(8,128)S(1)}, u32[]{:S(2)}, u32[]{:S(2)}) collective-permute-start(f32[2,40,128]{2,1,0:T(8,128)S(1)} %pad_maximum_fusion.1), channel_id=1, source_target_pairs={{0,4},{2,6},{4,0},{6,2},{8,12},{10,14},{12,8},{14,10},{1,5},{3,7},... | collective-permute-start | bytes 122888 | tf_op jit(solution)/shard_map/ppermute | solution.py:383
  24.3 9.3 %collective-permute-start.7 = (f32[8,40,128]{2,1,0:T(8,128)S(1)}, f32[8,40,128]{2,1,0:T(8,128)S(1)}, u32[]{:S(2)}, u32[]{:S(2)}) collective-permute-start(f32[8,40,128]{2,1,0:T(8,128)S(1)} %constant_dynamic-update-slice_fusion), channel_id=1, source_target_pairs={{0,1},{1,0},{2,3},{3,2},{4,5},{5,4},{6,7},{7,6},{8,9},{9,8},{10,11... | collective-permute-start | bytes 491528 | tf_op jit(solution)/shard_map/ppermute | solution.py:378
  24.4 6.3 %collective-permute-start.9 = (f32[2,32,256]{2,1,0:T(8,128)S(1)}, f32[2,32,256]{2,1,0:T(8,128)S(1)}, u32[]{:S(2)}, u32[]{:S(2)}) collective-permute-start(f32[2,32,256]{2,1,0:T(8,128)S(1)} %get-tuple-element.19), channel_id=1, source_target_pairs={{0,4},{2,14},{4,8},{6,2},{8,12},{10,6},{12,0},{14,10},{1,5},{3,15}... | collective-permute-start | bytes 196616 | tf_op jit(solution)/shard_map/ppermute | solution.py:383
  30.9 1.3 %collective-permute-start.10 = (f32[10,8,256]{2,1,0:T(8,128)S(1)}, f32[10,8,256]{2,1,0:T(8,128)S(1)}, u32[]{:S(2)}, u32[]{:S(2)}) collective-permute-start(f32[10,8,256]{2,1,0:T(8,128)S(1)} %get-tuple-element.21), channel_id=1, source_target_pairs={{0,1},{1,0},{2,3},{3,2},{4,5},{5,4},{6,7},{7,6},{8,9},{9,8},{10,11... | collective-permute-start | bytes 245768 | tf_op jit(solution)/shard_map/ppermute | solution.py:378
